TPU v7x, 32 devices: a whole 2x2x4 slice. The times are simulated.
32 devices in a mesh: dev: 8 (over z, y), rep: 4 (over x, core).
Axes of the slice: x: 2, y: 2, z: 4, core: 2. Of those that a mesh axis runs over, the one named last changes fastest.
Arguments:
- features: bfloat16 [32768, 256], P(('dev', 'rep')), may hold values from -6 to 6
- history: bfloat16 [32768, 256], P(('dev', 'rep')), may hold values from -6 to 6
- new_owner: int32 [32, 8], P(('dev', 'rep')), may hold values from 0 to 7, as said below
- pull_rows: int32 [32768], P(('dev', 'rep')), may hold values from 0 to 1023
- occupancy: int32 [256, 16], P(('dev', 'rep')), may hold values from 0 to 1, as said below
- adj_local: bfloat16 [32768, 1024], P(('dev', 'rep')), may hold values from -0.125 to 0.125
- adj_boundary: bfloat16 [32768, 1024], P(('dev', 'rep')), may hold values from -0.125 to 0.125
- w_first: bfloat16 [256, 256], replicated, may hold values from -0.375 to 0.375
- bias_first: float32 [256], replicated, may hold values from -3 to 3
- w_second: bfloat16 [256, 256], replicated, may hold values from -0.375 to 0.375
- cotangent: bfloat16 [32768, 256], P(('dev', 'rep')), may hold values from -6 to 6
Outputs:
- hidden: bfloat16 [32768, 256], P(('dev', 'rep'))
- output: bfloat16 [32768, 256], P(('dev', 'rep'))
- w_second_grad: float32 [256, 256], replicated
Inputs may be any that keep to these rules, and one draw needn't show every extreme that they name: Each row of new_owner is a permutation of 0 to 7. `occupancy`: tile flags of 0 or 1.
All inputs are finite; a program needn't handle non-finite values.
Results may differ from a plain program's by a relative error of at most 0.0061.
Values may be sent and summed in bfloat16 or wider, within the bound.
A program may use at most 64 MiB of HBM per device.

v0:
```python
import functools

import jax
import jax.numpy as jnp
from jax import lax
from jax.experimental import pallas as pl
from jax.experimental.pallas import tpu as pltpu
from jax.sharding import PartitionSpec as P

MESH = pl.DeviceIdType.MESH
F32 = jnp.float32
BF16 = jnp.bfloat16
ASK, MOVE_X, MOVE_H, FAR_X, FAR_H, PUSH_ONE, PUSH_TWO, SCATTER, GATHER = range(9)


def step_kernel(
    n,
    reps,
    features,
    history,
    new_owner,
    pulls,
    occupancy,
    adj_local_hbm,
    adj_edge_hbm,
    w_first,
    bias_first,
    w_second,
    cotangent_hbm,
    hidden_out,
    output_out,
    grad_out,
    local,
    edge,
    edge_t,
    cotangent,
    asked,
    pick,
    pick_t,
    send_x,
    send_h,
    own_x,
    own_h,
    send_far_x,
    send_far_h,
    far_x,
    far_h,
    send_one,
    send_two,
    push_one,
    push_two,
    acc,
    hidden,
    agg,
    grad_mine,
    grad_rep,
    sum_rep,
    grad_dev,
    sum_dev,
    grad_rows,
    grad_all,
    load_sem,
    send_sem,
    recv_sem,
    rep_send,
    rep_recv,
):
    me = lax.axis_index("dev")
    my_rep = lax.axis_index("rep")
    height, breadth = features.shape
    cluster = height // n
    per_peer = pulls.shape[2]
    pulled = n * per_peer
    tile = height // occupancy.shape[0]
    band = min(256, height)

    def peer(off):
        return lax.rem(me + off, n)

    def rep_peer(off):
        return lax.rem(my_rep + off, reps)

    loads = [
        pltpu.make_async_copy(adj_edge_hbm, edge, load_sem.at[0]),
        pltpu.make_async_copy(adj_local_hbm, local, load_sem.at[1]),
        pltpu.make_async_copy(cotangent_hbm, cotangent, load_sem.at[2]),
    ]
    for load in loads:
        load.start()

    barrier = pltpu.get_barrier_semaphore()
    for off in range(1, n):
        pl.semaphore_signal(barrier, inc=1, device_id={"dev": peer(off)}, device_id_type=MESH)
    for off in range(1, reps):
        pl.semaphore_signal(barrier, inc=1, device_id={"rep": rep_peer(off)}, device_id_type=MESH)

    def cluster_for(source, owner):
        block = jnp.zeros((cluster, breadth), BF16)
        for j in range(n):
            chosen = jnp.where(new_owner[0, j] == owner, 1.0, 0.0)
            weight = jnp.full((cluster, breadth), chosen, F32).astype(BF16)
            block = block + source[j * cluster : (j + 1) * cluster, :] * weight
        return block

    def outgoing(phase, src, dst, to, slot):
        return pltpu.make_async_remote_copy(
            src_ref=src.at[to],
            dst_ref=dst.at[slot],
            send_sem=send_sem.at[phase, to],
            recv_sem=recv_sem.at[phase, slot],
            device_id={"dev": to},
            device_id_type=MESH,
        )

    def send(phase, src, dst, off):
        outgoing(phase, src, dst, peer(off), me).start()

    def receive(phase, src, dst):
        for off in range(1, n):
            other = peer(off)
            outgoing(phase, src, dst, other, other).wait_recv()

    def finish(phase, src, dst):
        for off in range(1, n):
            outgoing(phase, src, dst, peer(off), me).wait_send()

    for off in range(1, n):
        send_x[peer(off)] = cluster_for(features, peer(off))
    own_x[me] = cluster_for(features, me)
    pl.semaphore_wait(barrier, n - 1 + reps - 1)
    for off in range(1, n):
        send(ASK, pulls, asked, off)
    for off in range(1, n):
        send(MOVE_X, send_x, own_x, off)
    for off in range(1, n):
        send_h[peer(off)] = cluster_for(history, peer(off))
        send(MOVE_H, send_h, own_h, off)
    own_h[me] = cluster_for(history, me)
    asked[me] = pulls[me]

    loads[0].wait()
    for i in range(height // tile):
        for j in range(pulled // tile):
            kept = occupancy[i, height // tile + j].astype(F32)
            rows, cols = pl.ds(i * tile, tile), pl.ds(j * tile, tile)
            part = (edge[rows, cols].astype(F32) * kept).astype(BF16)
            edge[rows, cols] = part
            edge_t[cols, rows] = part.T
    loads[1].wait()
    for i in range(height // tile):
        for j in range(height // tile):
            kept = occupancy[i, j].astype(F32)
            rows, cols = pl.ds(i * tile, tile), pl.ds(j * tile, tile)
            local[rows, cols] = (local[rows, cols].astype(F32) * kept).astype(BF16)

    receive(ASK, pulls, asked)
    for d in range(n):
        wanted = asked[d]
        rows = lax.broadcasted_iota(jnp.int32, (height, per_peer), 0)
        pick[:, d * per_peer : (d + 1) * per_peer] = jnp.where(rows == wanted, 1.0, 0.0).astype(
            BF16
        )
        turned = jnp.broadcast_to(wanted, (per_peer, per_peer)).T
        lanes = lax.broadcasted_iota(jnp.int32, (per_peer, per_peer), 1)
        for c in range(height // per_peer):
            pick_t[d * per_peer : (d + 1) * per_peer, c * per_peer : (c + 1) * per_peer] = (
                jnp.where(turned == lanes + c * per_peer, 1.0, 0.0).astype(BF16)
            )

    def blocks_out(phase, left, right, src, dst):
        values = right[...].reshape(left.shape[1], breadth)

        def block(to):
            rows = pl.ds(pl.multiple_of(to * per_peer, per_peer), per_peer)
            return jnp.dot(left[rows, :], values, preferred_element_type=F32).astype(BF16)

        def one(off, carry):
            src[peer(off)] = block(peer(off))
            send(phase, src, dst, off)
            return carry

        lax.fori_loop(1, n, one, 0)
        dst[me] = block(me)

    def bands(body):
        def one(i, carry):
            body(pl.ds(pl.multiple_of(i * band, band), band))
            return carry

        lax.fori_loop(0, height // band, one, 0)

    def times(left, rows, right):
        values = right[...].reshape(left.shape[1], breadth)
        return jnp.dot(left[rows, :], values, preferred_element_type=F32)

    receive(MOVE_X, send_x, own_x)
    blocks_out(FAR_X, pick_t, own_x, send_far_x, far_x)
    blocks_out(PUSH_ONE, edge_t, own_x, send_one, push_one)

    def local_one(rows):
        acc[rows, :] = times(local, rows, own_x)

    bands(local_one)
    receive(MOVE_H, send_h, own_h)
    blocks_out(FAR_H, pick_t, own_h, send_far_h, far_h)
    receive(FAR_X, send_far_x, far_x)

    def edge_one(rows):
        acc[rows, :] = acc[rows, :] + times(edge, rows, far_x)

    bands(edge_one)
    receive(PUSH_ONE, send_one, push_one)

    def first(rows):
        total = (acc[rows, :] + times(pick, rows, push_one)).astype(BF16)
        value = jnp.dot(total, w_first[...], preferred_element_type=F32) + bias_first[...]
        value = jnp.maximum(value, 0.0).astype(BF16)
        hidden[rows, :] = value
        hidden_out[rows, :] = value

    bands(first)
    blocks_out(PUSH_TWO, edge_t, hidden, send_two, push_two)

    def local_two(rows):
        acc[rows, :] = times(local, rows, hidden)

    bands(local_two)
    receive(FAR_H, send_far_h, far_h)

    def edge_two(rows):
        acc[rows, :] = acc[rows, :] + times(edge, rows, far_h)

    bands(edge_two)
    loads[2].wait()
    receive(PUSH_TWO, send_two, push_two)

    def second(rows):
        agg[rows, :] = (acc[rows, :] + times(pick, rows, push_two)).astype(BF16)

    bands(second)
    grad = lax.dot_general(
        agg[...], cotangent[...], (((0,), (0,)), ((), ())), preferred_element_type=F32
    )
    grad_mine[...] = grad.reshape(grad_mine.shape)

    def across(phase, src, dst, to, slot):
        return pltpu.make_async_remote_copy(
            src_ref=src,
            dst_ref=dst.at[slot],
            send_sem=rep_send.at[phase, to],
            recv_sem=rep_recv.at[phase, slot],
            device_id={"rep": to},
            device_id_type=MESH,
        )

    def share(src, dst, to, slot):
        return pltpu.make_async_remote_copy(
            src_ref=src,
            dst_ref=dst.at[slot],
            send_sem=send_sem.at[GATHER, to],
            recv_sem=recv_sem.at[GATHER, slot],
            device_id={"dev": to},
            device_id_type=MESH,
        )

    for off in range(1, reps):
        to = rep_peer(off)
        across(0, grad_mine.at[to], grad_rep, to, my_rep).start()

    def last(rows):
        output_out[rows, :] = jnp.dot(
            agg[rows, :], w_second[...], preferred_element_type=F32
        ).astype(BF16)

    bands(last)
    total = grad_mine[my_rep]
    for off in range(1, reps):
        to = rep_peer(off)
        across(0, grad_mine.at[to], grad_rep, to, to).wait_recv()
        total = total + grad_rep[to]
    sum_rep[...] = total
    for off in range(1, n):
        send(SCATTER, sum_rep, grad_dev, off)
    receive(SCATTER, sum_rep, grad_dev)
    grad_dev[me] = sum_rep[me]
    rows_sum = grad_dev[0]
    for d in range(1, n):
        rows_sum = rows_sum + grad_dev[d]
    sum_dev[...] = rows_sum
    for off in range(1, n):
        share(sum_dev, grad_rows, peer(off), me).start()
    grad_rows[me] = rows_sum
    for off in range(1, n):
        share(sum_dev, grad_rows, peer(off), peer(off)).wait_recv()
    for off in range(1, reps):
        across(1, grad_rows, grad_all, rep_peer(off), my_rep).start()
    grad_all[my_rep] = grad_rows[...]
    for off in range(1, reps):
        across(1, grad_rows, grad_all, rep_peer(off), rep_peer(off)).wait_recv()
    grad_out[...] = grad_all[...]

    finish(ASK, pulls, asked)
    finish(MOVE_X, send_x, own_x)
    finish(MOVE_H, send_h, own_h)
    finish(FAR_X, send_far_x, far_x)
    finish(FAR_H, send_far_h, far_h)
    finish(PUSH_ONE, send_one, push_one)
    finish(PUSH_TWO, send_two, push_two)
    finish(SCATTER, sum_rep, grad_dev)
    for off in range(1, n):
        share(sum_dev, grad_rows, peer(off), me).wait_send()
    for off in range(1, reps):
        to = rep_peer(off)
        across(0, grad_mine.at[to], grad_rep, to, my_rep).wait_send()
        across(1, grad_rows, grad_all, to, my_rep).wait_send()


def fused(
    features,
    history,
    new_owner,
    pull_rows,
    occupancy,
    adj_local,
    adj_boundary,
    w_first,
    bias_first,
    w_second,
    cotangent,
):
    n, reps = lax.axis_size("dev"), lax.axis_size("rep")
    height, breadth = features.shape
    cluster = height // n
    pulled = pull_rows.shape[0]
    per_peer = pulled // n
    part = breadth // (n * reps)
    vmem = pl.BlockSpec(memory_space=pltpu.VMEM)
    smem = pl.BlockSpec(memory_space=pltpu.SMEM)
    anywhere = pl.BlockSpec(memory_space=pl.ANY)
    moved = pltpu.VMEM((n, cluster, breadth), BF16)
    listed = pltpu.VMEM((n, per_peer, breadth), BF16)
    strip = pltpu.VMEM((n, part, breadth), F32)
    square = pltpu.VMEM((reps, n, part, breadth), F32)
    hidden, output, gradient = pl.pallas_call(
        functools.partial(step_kernel, n, reps),
        out_shape=(
            jax.ShapeDtypeStruct((height, breadth), BF16),
            jax.ShapeDtypeStruct((height, breadth), BF16),
            jax.ShapeDtypeStruct((reps, n, part, breadth), F32),
        ),
        in_specs=[
            vmem,
            vmem,
            smem,
            vmem,
            smem,
            anywhere,
            anywhere,
            vmem,
            vmem,
            vmem,
            anywhere,
        ],
        out_specs=(vmem, vmem, vmem),
        scratch_shapes=[
            pltpu.VMEM((height, height), BF16),
            pltpu.VMEM((height, pulled), BF16),
            pltpu.VMEM((pulled, height), BF16),
            pltpu.VMEM((height, breadth), BF16),
            pltpu.VMEM((n, 1, per_peer), jnp.int32),
            pltpu.VMEM((height, pulled), BF16),
            pltpu.VMEM((pulled, height), BF16),
            moved,
            moved,
            moved,
            moved,
            listed,
            listed,
            listed,
            listed,
            listed,
            listed,
            listed,
            listed,
            pltpu.VMEM((height, breadth), F32),
            pltpu.VMEM((height, breadth), BF16),
            pltpu.VMEM((height, breadth), BF16),
            square,
            square,
            strip,
            strip,
            pltpu.VMEM((part, breadth), F32),
            strip,
            square,
            pltpu.SemaphoreType.DMA((3,)),
            pltpu.SemaphoreType.DMA((9, n)),
            pltpu.SemaphoreType.DMA((9, n)),
            pltpu.SemaphoreType.DMA((2, reps)),
            pltpu.SemaphoreType.DMA((2, reps)),
        ],
        compiler_params=pltpu.CompilerParams(
            collective_id=0, has_side_effects=True, vmem_limit_bytes=56 * 1024 * 1024
        ),
    )(
        features,
        history,
        new_owner,
        pull_rows.reshape(n, 1, per_peer),
        occupancy,
        adj_local,
        adj_boundary,
        w_first,
        bias_first.reshape(1, breadth),
        w_second,
        cotangent,
    )
    return hidden, output, gradient.reshape(breadth, breadth)


def fits(peers, height, pulled, breadth, everyone):
    return (
        height % (128 * peers) == 0 and pulled == 128 * peers and breadth % (8 * everyone) == 0
    )


def expand(occupied):
    return jnp.repeat(jnp.repeat(occupied, 128, axis=0), 128, axis=1).astype(jnp.bfloat16)


def dense_terms(owned, remote, adj_local, adj_boundary, occupancy):
    height = owned.shape[0]
    full_mask = expand(occupancy)
    local_tile = adj_local * full_mask[:, :height]
    edge_tile = adj_boundary * full_mask[:, height:]
    summed = jnp.dot(local_tile, owned, preferred_element_type=jnp.float32)
    summed = summed + jnp.dot(edge_tile, remote, preferred_element_type=jnp.float32)
    partial_value = lax.dot_general(
        edge_tile, owned, (((0,), (0,)), ((), ())), preferred_element_type=jnp.float32
    )
    return (summed, partial_value)


def body(
    features,
    history,
    new_owner,
    pull_rows,
    occupancy,
    adj_local,
    adj_boundary,
    w_first,
    bias_first,
    w_second,
    cotangent,
):
    peer_count = lax.axis_size("dev")
    height, breadth = features.shape
    cluster = height // peer_count
    pulled = pull_rows.shape[0]
    per_peer = pulled // peer_count
    everyone = peer_count * lax.axis_size("rep")
    if fits(peer_count, height, pulled, breadth, everyone):
        return fused(
            features,
            history,
            new_owner,
            pull_rows,
            occupancy,
            adj_local,
            adj_boundary,
            w_first,
            bias_first,
            w_second,
            cotangent,
        )
    indices = jnp.arange(peer_count, dtype=jnp.int32)
    matches = (new_owner[0][:, None] == indices[None, :]).astype(jnp.int32)
    inverse = jnp.sum(matches * indices[:, None], axis=0)

    def arrange(values):
        return values.reshape(peer_count, cluster, breadth)[inverse]

    requests = lax.all_to_all(
        pull_rows.reshape(peer_count, per_peer), "dev", split_axis=0, concat_axis=0, tiled=True
    ).reshape(pulled)

    def fetch_rows(values):
        return values[requests].reshape(peer_count, per_peer, breadth)

    selector = (requests[None, :] == jnp.arange(height, dtype=jnp.int32)[:, None]).astype(
        jnp.bfloat16
    )

    def collect(received):
        return jnp.dot(
            selector, received.reshape(pulled, breadth), preferred_element_type=jnp.float32
        )

    def layer_terms(owned, remote):
        return dense_terms(owned, remote, adj_local, adj_boundary, occupancy)

    moved_x, moved_h = (
        lax.all_to_all(arrange(features), "dev", split_axis=0, concat_axis=0, tiled=True),
        lax.all_to_all(arrange(history), "dev", split_axis=0, concat_axis=0, tiled=True),
    )
    own_x = moved_x.reshape(height, breadth)
    own_h = moved_h.reshape(height, breadth)
    far_x, far_h = (
        lax.all_to_all(fetch_rows(own_x), "dev", split_axis=0, concat_axis=0, tiled=True),
        lax.all_to_all(fetch_rows(own_h), "dev", split_axis=0, concat_axis=0, tiled=True),
    )
    summed_one, partial_one = layer_terms(own_x, far_x.reshape(pulled, breadth))
    pushed_one = lax.all_to_all(
        partial_one.astype(jnp.bfloat16).reshape(peer_count, per_peer, breadth),
        "dev",
        split_axis=0,
        concat_axis=0,
        tiled=True,
    )
    far_h = far_h.reshape(pulled, breadth)
    aggregate_one = (summed_one + collect(pushed_one)).astype(jnp.bfloat16)
    hidden = jnp.maximum(
        jnp.dot(aggregate_one, w_first, preferred_element_type=jnp.float32) + bias_first, 0.0
    ).astype(jnp.bfloat16)
    summed_two, partial_two = layer_terms(hidden, far_h)
    pushed_two = lax.all_to_all(
        partial_two.astype(jnp.bfloat16).reshape(peer_count, per_peer, breadth),
        "dev",
        split_axis=0,
        concat_axis=0,
        tiled=True,
    )
    aggregate_two = (summed_two + collect(pushed_two)).astype(jnp.bfloat16)
    output = jnp.dot(aggregate_two, w_second, preferred_element_type=jnp.float32).astype(
        jnp.bfloat16
    )
    local_grad = lax.dot_general(
        aggregate_two, cotangent, (((0,), (0,)), ((), ())), preferred_element_type=jnp.float32
    )
    slices = lax.all_to_all(
        local_grad.reshape(everyone, breadth // everyone, breadth),
        ("dev", "rep"),
        split_axis=0,
        concat_axis=0,
        tiled=True,
    )
    gradient = lax.all_gather(jnp.sum(slices, axis=0), ("dev", "rep"), axis=0, tiled=True)
    return (hidden, output, gradient)


def solution(mesh):
    return jax.shard_map(
        body,
        mesh=mesh,
        in_specs=(
            P(("dev", "rep"), None),
            P(("dev", "rep"), None),
            P(("dev", "rep"), None),
            P(("dev", "rep")),
            P(("dev", "rep"), None),
            P(("dev", "rep"), None),
            P(("dev", "rep"), None),
            P(),
            P(),
            P(),
            P(("dev", "rep"), None),
        ),
        out_specs=(P(("dev", "rep"), None), P(("dev", "rep"), None), P()),
        check_vma=False,
    )
```

profile of v0, /device:TPU:0, one launch (start us, length us, event | category | flops | bytes accessed | tf_op | source)
XLA Modules:
  0.0 99.9 jit_solution(6996259685583810523)
XLA Ops:
  0.6 94.8 %shard_map.130 = (bf16[1024,256]{1,0:T(8,128)(2,1)}, bf16[1024,256]{1,0:T(8,128)(2,1)}, f32[4,8,8,256]{3,2,1,0:T(8,128)}) custom-call(bf16[1024,256]{1,0:T(8,128)(2,1)} %features.1, bf16[1024,256]{1,0:T(8,128)(2,1)} %history.1, s32[1,8]{1,0:T(1,128)} %new_owner.1, s32[8,1,128]{2,1,0:T(1,128)} %bitcast.4, s32[8,16]{1,0:T(8,128)} %occupancy.1, ...), custom_call_target="tpu_custom_call" | custom-call | tf_op jit(solution)/shard_map/pallas_call | solution.py:344
  95.4 0.0 copy-start
  95.4 1.9 %copy.17 = bf16[1024,256]{1,0:T(8,128)(2,1)} copy(bf16[1024,256]{1,0:T(8,128)(2,1)} %get-tuple-element.12) | data formatting | bytes 1048576
  97.3 1.9 %copy.18 = bf16[1024,256]{1,0:T(8,128)(2,1)} copy(bf16[1024,256]{1,0:T(8,128)(2,1)} %get-tuple-element.13) | data formatting | bytes 1048576
  99.2 0.0 copy-done
  99.2 0.7 copy.19
Async XLA Ops:
  95.4 3.8 %copy-start = (f32[4,8,8,256]{3,2,1,0:T(8,128)S(1)}, f32[4,8,8,256]{3,2,1,0:T(8,128)}, u32[]{:S(2)}) copy-start(f32[4,8,8,256]{3,2,1,0:T(8,128)} %get-tuple-element.8) | copy-start | bytes 786436
where the time goes:
time: 100 us; the launch traced here: 99.9 us
  Pallas kernels  94.8 us (95%)
  local copies, waits for them, and re-layouts  4.48 us (4%)
    pallas_call x1, Pallas kernels, fused(): pl.pallas_call(functools.partial(step_kernel, n, reps), out_shape=(jax.Sh...  94.8 us
    unnamed x5, local copies, waits for them, and re-layouts  4.48 us

commit v1 on v0

--- a/solution.py
+++ b/solution.py
@@ -10,26 +10,35 @@
 MESH = pl.DeviceIdType.MESH
 F32 = jnp.float32
 BF16 = jnp.bfloat16
-ASK, MOVE_X, MOVE_H, FAR_X, FAR_H, PUSH_ONE, PUSH_TWO, SCATTER, GATHER = range(9)
+ASK, MOVE_X, MOVE_H, FAR_X, FAR_H, PUSH_ONE, PUSH_TWO = range(7)
 
 
 def step_kernel(
     n,
     reps,
+    inner,
+    features_hbm,
+    history_hbm,
+    new_owner_hbm,
+    pulls_hbm,
+    occupancy_hbm,
+    adj_local_hbm,
+    adj_edge_hbm,
+    w_first_hbm,
+    bias_first_hbm,
+    w_second_hbm,
+    cotangent_hbm,
+    hidden,
+    output_out,
+    grad_out,
     features,
     history,
     new_owner,
     pulls,
     occupancy,
-    adj_local_hbm,
-    adj_edge_hbm,
     w_first,
     bias_first,
     w_second,
-    cotangent_hbm,
-    hidden_out,
-    output_out,
-    grad_out,
     local,
     edge,
     edge_t,
@@ -50,20 +59,20 @@
     push_one,
     push_two,
     acc,
-    hidden,
     agg,
     grad_mine,
-    grad_rep,
-    sum_rep,
-    grad_dev,
-    sum_dev,
-    grad_rows,
+    grad_near,
+    strip_mine,
+    strip_far,
+    total_mine,
     grad_all,
     load_sem,
     send_sem,
     recv_sem,
-    rep_send,
-    rep_recv,
+    near_send,
+    near_recv,
+    far_send,
+    far_recv,
 ):
     me = lax.axis_index("dev")
     my_rep = lax.axis_index("rep")
@@ -80,19 +89,58 @@
     def rep_peer(off):
         return lax.rem(my_rep + off, reps)
 
+    everyone = inner * reps
+    outer = n // inner
+    line = me // inner
+    spot = lax.rem(me, inner) * reps + my_rep
+
+    def near(off):
+        return lax.rem(spot + off, everyone)
+
+    def near_id(at):
+        return {"dev": line * inner + at // reps, "rep": lax.rem(at, reps)}
+
+    def far(off):
+        return lax.rem(line + off, outer)
+
+    def far_id(at):
+        return {"dev": at * inner + lax.rem(me, inner)}
+
+    barrier = pltpu.get_barrier_semaphore()
+    for off in range(1, n):
+        pl.semaphore_signal(barrier, inc=1, device_id={"dev": peer(off)}, device_id_type=MESH)
+    for side in range(inner):
+        for off in range(1, reps):
+            pl.semaphore_signal(
+                barrier,
+                inc=1,
+                device_id={
+                    "dev": line * inner + lax.rem(me + side, inner),
+                    "rep": rep_peer(off),
+                },
+                device_id_type=MESH,
+            )
+
     loads = [
-        pltpu.make_async_copy(adj_edge_hbm, edge, load_sem.at[0]),
-        pltpu.make_async_copy(adj_local_hbm, local, load_sem.at[1]),
-        pltpu.make_async_copy(cotangent_hbm, cotangent, load_sem.at[2]),
+        pltpu.make_async_copy(source, target, load_sem.at[i])
+        for i, (source, target) in enumerate(
+            (
+                (new_owner_hbm, new_owner),
+                (features_hbm, features),
+                (pulls_hbm, pulls),
+                (history_hbm, history),
+                (occupancy_hbm, occupancy),
+                (adj_edge_hbm, edge),
+                (adj_local_hbm, local),
+                (w_first_hbm, w_first),
+                (bias_first_hbm, bias_first),
+                (w_second_hbm, w_second),
+                (cotangent_hbm, cotangent),
+            )
+        )
     ]
     for load in loads:
         load.start()
-
-    barrier = pltpu.get_barrier_semaphore()
-    for off in range(1, n):
-        pl.semaphore_signal(barrier, inc=1, device_id={"dev": peer(off)}, device_id_type=MESH)
-    for off in range(1, reps):
-        pl.semaphore_signal(barrier, inc=1, device_id={"rep": rep_peer(off)}, device_id_type=MESH)
 
     def cluster_for(source, owner):
         block = jnp.zeros((cluster, breadth), BF16)
@@ -124,21 +172,26 @@
         for off in range(1, n):
             outgoing(phase, src, dst, peer(off), me).wait_send()
 
+    loads[0].wait()
+    loads[1].wait()
     for off in range(1, n):
         send_x[peer(off)] = cluster_for(features, peer(off))
     own_x[me] = cluster_for(features, me)
-    pl.semaphore_wait(barrier, n - 1 + reps - 1)
+    loads[2].wait()
+    pl.semaphore_wait(barrier, n - 1 + inner * (reps - 1))
     for off in range(1, n):
         send(ASK, pulls, asked, off)
     for off in range(1, n):
         send(MOVE_X, send_x, own_x, off)
+    loads[3].wait()
     for off in range(1, n):
         send_h[peer(off)] = cluster_for(history, peer(off))
         send(MOVE_H, send_h, own_h, off)
     own_h[me] = cluster_for(history, me)
     asked[me] = pulls[me]
 
-    loads[0].wait()
+    loads[4].wait()
+    loads[5].wait()
     for i in range(height // tile):
         for j in range(pulled // tile):
             kept = occupancy[i, height // tile + j].astype(F32)
@@ -146,7 +199,7 @@
             part = (edge[rows, cols].astype(F32) * kept).astype(BF16)
             edge[rows, cols] = part
             edge_t[cols, rows] = part.T
-    loads[1].wait()
+    loads[6].wait()
     for i in range(height // tile):
         for j in range(height // tile):
             kept = occupancy[i, j].astype(F32)
@@ -216,8 +269,9 @@
         value = jnp.dot(total, w_first[...], preferred_element_type=F32) + bias_first[...]
         value = jnp.maximum(value, 0.0).astype(BF16)
         hidden[rows, :] = value
-        hidden_out[rows, :] = value
-
+
+    loads[7].wait()
+    loads[8].wait()
     bands(first)
     blocks_out(PUSH_TWO, edge_t, hidden, send_two, push_two)
 
@@ -231,7 +285,8 @@
         acc[rows, :] = acc[rows, :] + times(edge, rows, far_h)
 
     bands(edge_two)
-    loads[2].wait()
+    loads[9].wait()
+    loads[10].wait()
     receive(PUSH_TWO, send_two, push_two)
 
     def second(rows):
@@ -241,31 +296,30 @@
     grad = lax.dot_general(
         agg[...], cotangent[...], (((0,), (0,)), ((), ())), preferred_element_type=F32
     )
-    grad_mine[...] = grad.reshape(grad_mine.shape)
-
-    def across(phase, src, dst, to, slot):
+    grad_mine[...] = grad.reshape(grad_mine.shape).astype(BF16)
+
+    def near_copy(phase, src, dst, to, slot):
         return pltpu.make_async_remote_copy(
             src_ref=src,
             dst_ref=dst.at[slot],
-            send_sem=rep_send.at[phase, to],
-            recv_sem=rep_recv.at[phase, slot],
-            device_id={"rep": to},
+            send_sem=near_send.at[phase, to],
+            recv_sem=near_recv.at[phase, slot],
+            device_id=near_id(to),
             device_id_type=MESH,
         )
 
-    def share(src, dst, to, slot):
+    def far_copy(to, slot):
         return pltpu.make_async_remote_copy(
-            src_ref=src,
-            dst_ref=dst.at[slot],
-            send_sem=send_sem.at[GATHER, to],
-            recv_sem=recv_sem.at[GATHER, slot],
-            device_id={"dev": to},
+            src_ref=strip_mine,
+            dst_ref=strip_far.at[slot],
+            send_sem=far_send.at[to],
+            recv_sem=far_recv.at[slot],
+            device_id=far_id(to),
             device_id_type=MESH,
         )
 
-    for off in range(1, reps):
-        to = rep_peer(off)
-        across(0, grad_mine.at[to], grad_rep, to, my_rep).start()
+    for off in range(1, everyone):
+        near_copy(0, grad_mine.at[near(off)], grad_near, near(off), spot).start()
 
     def last(rows):
         output_out[rows, :] = jnp.dot(
@@ -273,31 +327,26 @@
         ).astype(BF16)
 
     bands(last)
-    total = grad_mine[my_rep]
-    for off in range(1, reps):
-        to = rep_peer(off)
-        across(0, grad_mine.at[to], grad_rep, to, to).wait_recv()
-        total = total + grad_rep[to]
-    sum_rep[...] = total
-    for off in range(1, n):
-        send(SCATTER, sum_rep, grad_dev, off)
-    receive(SCATTER, sum_rep, grad_dev)
-    grad_dev[me] = sum_rep[me]
-    rows_sum = grad_dev[0]
-    for d in range(1, n):
-        rows_sum = rows_sum + grad_dev[d]
-    sum_dev[...] = rows_sum
-    for off in range(1, n):
-        share(sum_dev, grad_rows, peer(off), me).start()
-    grad_rows[me] = rows_sum
-    for off in range(1, n):
-        share(sum_dev, grad_rows, peer(off), peer(off)).wait_recv()
-    for off in range(1, reps):
-        across(1, grad_rows, grad_all, rep_peer(off), my_rep).start()
-    grad_all[my_rep] = grad_rows[...]
-    for off in range(1, reps):
-        across(1, grad_rows, grad_all, rep_peer(off), rep_peer(off)).wait_recv()
-    grad_out[...] = grad_all[...]
+    total = grad_mine[spot].astype(F32)
+    for off in range(1, everyone):
+        near_copy(0, grad_mine.at[near(off)], grad_near, near(off), near(off)).wait_recv()
+        total = total + grad_near[near(off)].astype(F32)
+    strip_mine[...] = total.astype(BF16)
+    for off in range(1, outer):
+        far_copy(far(off), line).start()
+    strip_far[line] = strip_mine[...]
+    for off in range(1, outer):
+        far_copy(far(off), far(off)).wait_recv()
+    total = strip_far[0].astype(F32)
+    for z in range(1, outer):
+        total = total + strip_far[z].astype(F32)
+    total_mine[...] = total.astype(BF16)
+    for off in range(1, everyone):
+        near_copy(1, total_mine, grad_all, near(off), spot).start()
+    grad_all[spot] = total_mine[...]
+    for off in range(1, everyone):
+        near_copy(1, total_mine, grad_all, near(off), near(off)).wait_recv()
+    grad_out[...] = grad_all[...].astype(F32).reshape(grad_out.shape)
 
     finish(ASK, pulls, asked)
     finish(MOVE_X, send_x, own_x)
@@ -306,13 +355,34 @@
     finish(FAR_H, send_far_h, far_h)
     finish(PUSH_ONE, send_one, push_one)
     finish(PUSH_TWO, send_two, push_two)
-    finish(SCATTER, sum_rep, grad_dev)
-    for off in range(1, n):
-        share(sum_dev, grad_rows, peer(off), me).wait_send()
-    for off in range(1, reps):
-        to = rep_peer(off)
-        across(0, grad_mine.at[to], grad_rep, to, my_rep).wait_send()
-        across(1, grad_rows, grad_all, to, my_rep).wait_send()
+    for off in range(1, everyone):
+        near_copy(0, grad_mine.at[near(off)], grad_near, near(off), spot).wait_send()
+        near_copy(1, total_mine, grad_all, near(off), spot).wait_send()
+    for off in range(1, outer):
+        far_copy(far(off), line).wait_send()
+
+
+def store_kernel(count, *refs):
+    sems = refs[-1]
+    copies = [
+        pltpu.make_async_copy(refs[i], refs[count + i], sems.at[i]) for i in range(count)
+    ]
+    for copy in copies:
+        copy.start()
+    for copy in copies:
+        copy.wait()
+
+
+def store(*values):
+    count = len(values)
+    return pl.pallas_call(
+        functools.partial(store_kernel, count),
+        out_shape=tuple(jax.ShapeDtypeStruct(v.shape, v.dtype) for v in values),
+        in_specs=[pl.BlockSpec(memory_space=pltpu.VMEM)] * count,
+        out_specs=tuple(pl.BlockSpec(memory_space=pl.ANY) for _ in values),
+        scratch_shapes=[pltpu.SemaphoreType.DMA((count,))],
+        compiler_params=pltpu.CompilerParams(vmem_limit_bytes=8 * 1024 * 1024),
+    )(*values)
 
 
 def fused(
@@ -333,40 +403,39 @@
     cluster = height // n
     pulled = pull_rows.shape[0]
     per_peer = pulled // n
-    part = breadth // (n * reps)
+    inner = near_width(n)
+    everyone = inner * reps
+    part = breadth // everyone
     vmem = pl.BlockSpec(memory_space=pltpu.VMEM)
-    smem = pl.BlockSpec(memory_space=pltpu.SMEM)
-    anywhere = pl.BlockSpec(memory_space=pl.ANY)
+    anywhere = pl.BlockSpec(memory_space=pltpu.HBM)
     moved = pltpu.VMEM((n, cluster, breadth), BF16)
     listed = pltpu.VMEM((n, per_peer, breadth), BF16)
-    strip = pltpu.VMEM((n, part, breadth), F32)
-    square = pltpu.VMEM((reps, n, part, breadth), F32)
-    hidden, output, gradient = pl.pallas_call(
-        functools.partial(step_kernel, n, reps),
+    square = pltpu.VMEM((everyone, part, breadth), BF16)
+    strip = pltpu.VMEM((part, breadth), BF16)
+    weight = pltpu.VMEM((breadth, breadth), BF16)
+    nodes = pltpu.VMEM((height, breadth), BF16)
+    results = pl.pallas_call(
+        functools.partial(step_kernel, n, reps, inner),
         out_shape=(
-            jax.ShapeDtypeStruct((height, breadth), BF16),
-            jax.ShapeDtypeStruct((height, breadth), BF16),
-            jax.ShapeDtypeStruct((reps, n, part, breadth), F32),
+            pltpu.VMEM((height, breadth), BF16),
+            pltpu.VMEM((height, breadth), BF16),
+            pltpu.VMEM((breadth, breadth), F32),
         ),
-        in_specs=[
-            vmem,
-            vmem,
-            smem,
-            vmem,
-            smem,
-            anywhere,
-            anywhere,
-            vmem,
-            vmem,
-            vmem,
-            anywhere,
-        ],
+        in_specs=[anywhere] * 11,
         out_specs=(vmem, vmem, vmem),
         scratch_shapes=[
+            nodes,
+            nodes,
+            pltpu.SMEM(new_owner.shape, jnp.int32),
+            pltpu.VMEM((n, 1, per_peer), jnp.int32),
+            pltpu.SMEM(occupancy.shape, jnp.int32),
+            weight,
+            pltpu.VMEM((1, breadth), F32),
+            weight,
             pltpu.VMEM((height, height), BF16),
             pltpu.VMEM((height, pulled), BF16),
             pltpu.VMEM((pulled, height), BF16),
-            pltpu.VMEM((height, breadth), BF16),
+            nodes,
             pltpu.VMEM((n, 1, per_peer), jnp.int32),
             pltpu.VMEM((height, pulled), BF16),
             pltpu.VMEM((pulled, height), BF16),
@@ -383,43 +452,54 @@
             listed,
             listed,
             pltpu.VMEM((height, breadth), F32),
-            pltpu.VMEM((height, breadth), BF16),
-            pltpu.VMEM((height, breadth), BF16),
+            nodes,
             square,
             square,
             strip,
-            strip,
-            pltpu.VMEM((part, breadth), F32),
+            pltpu.VMEM((n // inner, part, breadth), BF16),
             strip,
             square,
-            pltpu.SemaphoreType.DMA((3,)),
-            pltpu.SemaphoreType.DMA((9, n)),
-            pltpu.SemaphoreType.DMA((9, n)),
-            pltpu.SemaphoreType.DMA((2, reps)),
-            pltpu.SemaphoreType.DMA((2, reps)),
+            pltpu.SemaphoreType.DMA((11,)),
+            pltpu.SemaphoreType.DMA((7, n)),
+            pltpu.SemaphoreType.DMA((7, n)),
+            pltpu.SemaphoreType.DMA((2, everyone)),
+            pltpu.SemaphoreType.DMA((2, everyone)),
+            pltpu.SemaphoreType.DMA((n // inner,)),
+            pltpu.SemaphoreType.DMA((n // inner,)),
         ],
         compiler_params=pltpu.CompilerParams(
-            collective_id=0, has_side_effects=True, vmem_limit_bytes=56 * 1024 * 1024
+            collective_id=0, has_side_effects=True, vmem_limit_bytes=40 * 1024 * 1024
         ),
     )(
-        features,
-        history,
-        new_owner,
-        pull_rows.reshape(n, 1, per_peer),
-        occupancy,
-        adj_local,
-        adj_boundary,
-        w_first,
-        bias_first.reshape(1, breadth),
-        w_second,
-        cotangent,
-    )
-    return hidden, output, gradient.reshape(breadth, breadth)
-
-
-def fits(peers, height, pulled, breadth, everyone):
+        *(
+            pltpu.with_memory_space_constraint(value, pltpu.HBM)
+            for value in (
+                features,
+                history,
+                new_owner,
+                pull_rows.reshape(n, 1, per_peer),
+                occupancy,
+                adj_local,
+                adj_boundary,
+                w_first,
+                bias_first.reshape(1, breadth),
+                w_second,
+                cotangent,
+            )
+        )
+    )
+    return store(*results)
+
+
+def near_width(n):
+    return 2 if n % 2 == 0 else 1
+
+
+def fits(peers, height, pulled, breadth, reps):
     return (
-        height % (128 * peers) == 0 and pulled == 128 * peers and breadth % (8 * everyone) == 0
+        height % (128 * peers) == 0
+        and pulled == 128 * peers
+        and breadth % (16 * near_width(peers) * reps) == 0
     )
 
 
@@ -459,7 +539,7 @@
     pulled = pull_rows.shape[0]
     per_peer = pulled // peer_count
     everyone = peer_count * lax.axis_size("rep")
-    if fits(peer_count, height, pulled, breadth, everyone):
+    if fits(peer_count, height, pulled, breadth, lax.axis_size("rep")):
         return fused(
             features,
             history,

time: 100 us -> 90.8 us (0.908)
  Pallas kernels: 94.8 us -> 90 us
  local copies, waits for them, and re-layouts: 4.48 us -> 0 us
    pallas_call x1 -> x2, Pallas kernels: 94.8 us -> 90 us  [the longest x1 88.9 us: fused(): pl.pallas_call(functools.partial(step_kernel, n, reps, inner), out_shape=...]
    unnamed x5 -> x0, local copies, waits for them, and re-layouts: 4.48 us -> none
where the time goes in v1:
time: 90.8 us; the launch traced here: 90.6 us
  Pallas kernels  90 us (99%)
    pallas_call x1, Pallas kernels, fused(): pl.pallas_call(functools.partial(step_kernel, n, reps, inner), out_shape=...  88.9 us

profile of v1, /device:TPU:0, one launch (start us, length us, event | category | flops | bytes accessed | tf_op | source)
XLA Modules:
  0.0 90.6 jit_solution(8516565067208924629)
XLA Ops:
  0.6 88.9 %shard_map.130 = (bf16[1024,256]{1,0:T(8,128)(2,1)S(1)}, bf16[1024,256]{1,0:T(8,128)(2,1)S(1)}, f32[256,256]{1,0:T(8,128)S(1)}) custom-call(bf16[1024,256]{1,0:T(8,128)(2,1)} %features_hbm.1, bf16[1024,256]{1,0:T(8,128)(2,1)} %history_hbm.1, s32[1,8]{1,0:T(1,128)} %new_owner_hbm.1, s32[8,1,128]{2,1,0:T(1,128)} %bitcast.2, s32[8,16]{1,0:T(8,128)} %occupancy_hbm.1, ...), custom_call_target="tpu_custom_call" | custom-call | tf_op jit(solution)/shard_map/pallas_call | solution.py:417
  89.6 1.1 %shard_map.131 = (bf16[1024,256]{1,0:T(8,128)(2,1)}, bf16[1024,256]{1,0:T(8,128)(2,1)}, f32[256,256]{1,0:T(8,128)}) custom-call(bf16[1024,256]{1,0:T(8,128)(2,1)S(1)} %get-tuple-element.6.refs_0_, bf16[1024,256]{1,0:T(8,128)(2,1)S(1)} %get-tuple-element.7.refs_1_, f32[256,256]{1,0:T(8,128)S(1)} %get-tuple-element.8.refs_2_), custom_call_target="tpu_custom_call" | custom-call | tf_op jit(solution)/shard_map/pallas_call | solution.py:378

commit v2 on v1

--- a/solution.py
+++ b/solution.py
@@ -10,7 +10,7 @@
 MESH = pl.DeviceIdType.MESH
 F32 = jnp.float32
 BF16 = jnp.bfloat16
-ASK, MOVE_X, MOVE_H, FAR_X, FAR_H, PUSH_ONE, PUSH_TWO = range(7)
+ASK, ASK_H, MOVE_X, FAR_X, H_ONE, H_TWO, PUSH_ONE, PUSH_TWO = range(8)
 
 
 def step_kernel(
@@ -21,6 +21,7 @@
     history_hbm,
     new_owner_hbm,
     pulls_hbm,
+    lists_hbm,
     occupancy_hbm,
     adj_local_hbm,
     adj_edge_hbm,
@@ -31,10 +32,12 @@
     hidden,
     output_out,
     grad_out,
+    flag_out,
     features,
     history,
     new_owner,
     pulls,
+    lists,
     occupancy,
     w_first,
     bias_first,
@@ -44,15 +47,19 @@
     edge_t,
     cotangent,
     asked,
+    codes,
+    asked_h,
     pick,
     pick_t,
+    pick_h,
+    place,
     send_x,
-    send_h,
+    by_owner,
     own_x,
-    own_h,
     send_far_x,
-    send_far_h,
+    send_rows,
     far_x,
+    rows_in,
     far_h,
     send_one,
     send_two,
@@ -66,6 +73,8 @@
     strip_far,
     total_mine,
     grad_all,
+    flag_mine,
+    flag_all,
     load_sem,
     send_sem,
     recv_sem,
@@ -73,6 +82,8 @@
     near_recv,
     far_send,
     far_recv,
+    flag_send,
+    flag_recv,
 ):
     me = lax.axis_index("dev")
     my_rep = lax.axis_index("rep")
@@ -82,6 +93,9 @@
     pulled = n * per_peer
     tile = height // occupancy.shape[0]
     band = min(256, height)
+    room = send_rows.shape[1]
+    early = early_rows(room)
+    wide = codes.shape[2] - per_peer
 
     def peer(off):
         return lax.rem(me + off, n)
@@ -127,6 +141,7 @@
             (
                 (new_owner_hbm, new_owner),
                 (features_hbm, features),
+                (lists_hbm, lists),
                 (pulls_hbm, pulls),
                 (history_hbm, history),
                 (occupancy_hbm, occupancy),
@@ -172,26 +187,130 @@
         for off in range(1, n):
             outgoing(phase, src, dst, peer(off), me).wait_send()
 
+    def slots():
+        upper = jnp.where(
+            lax.broadcasted_iota(jnp.int32, (per_peer, per_peer), 0)
+            <= lax.broadcasted_iota(jnp.int32, (per_peer, per_peer), 1),
+            1.0,
+            0.0,
+        ).astype(BF16)
+        origin = lax.broadcasted_iota(jnp.int32, (n, per_peer), 0)
+        seats = lax.broadcasted_iota(jnp.int32, (wide, per_peer), 0).astype(F32)
+        held, within = [], []
+        for e in range(n):
+            row = jnp.broadcast_to(lists[e : e + 1, :], (n, per_peer)) - origin * cluster
+            held.append(jnp.where((row >= 0) & (row < cluster), 1.0, 0.0))
+            within.append(row.astype(F32))
+        stacked = jnp.concatenate(held, axis=0).astype(BF16)
+        prefix = jnp.dot(stacked, upper, preferred_element_type=F32)
+        totals = jnp.dot(
+            stacked, jnp.ones((per_peer, per_peer), BF16), preferred_element_type=F32
+        )
+        before = jnp.full((n, per_peer), -1.0, F32)
+        over = jnp.zeros((n, per_peer), F32)
+        table = jnp.zeros((2 * n, wide), F32)
+        places = []
+        for e in range(n):
+            seat = held[e] * (prefix[e * n : (e + 1) * n, :] + before)
+            before = before + totals[e * n : (e + 1) * n, :]
+            over = jnp.maximum(over, seat)
+            places.append(
+                jnp.sum(seat + held[e] * (origin * room).astype(F32), axis=0, keepdims=True)
+            )
+            mine = jnp.sum(seat, axis=0, keepdims=True)
+            taken = jnp.where(seats == mine, 1.0, 0.0).astype(BF16)
+            entry = jnp.concatenate([held[e] * float(e), held[e] * within[e]], axis=0)
+            table = table + lax.dot_general(
+                entry.astype(BF16), taken, (((1,), (1,)), ((), ())), preferred_element_type=F32
+            )
+        found = (table[:n, :] * float(cluster) + table[n:, :]).astype(jnp.int32)
+        full = jnp.where(jnp.max(over, axis=0, keepdims=True) >= float(room), 1, 0)
+        for d in range(n):
+            codes[d, :, :wide] = found[d : d + 1, :]
+            codes[d, :, wide:] = full
+        return places
+
+    loads[2].wait()
+    places = slots()
     loads[0].wait()
     loads[1].wait()
     for off in range(1, n):
         send_x[peer(off)] = cluster_for(features, peer(off))
     own_x[me] = cluster_for(features, me)
-    loads[2].wait()
+    loads[3].wait()
     pl.semaphore_wait(barrier, n - 1 + inner * (reps - 1))
+    for off in range(1, n):
+        send(ASK_H, codes, asked_h, off)
     for off in range(1, n):
         send(ASK, pulls, asked, off)
     for off in range(1, n):
         send(MOVE_X, send_x, own_x, off)
-    loads[3].wait()
-    for off in range(1, n):
-        send_h[peer(off)] = cluster_for(history, peer(off))
-        send(MOVE_H, send_h, own_h, off)
-    own_h[me] = cluster_for(history, me)
     asked[me] = pulls[me]
-
+    asked_h[me] = codes[me]
     loads[4].wait()
+    for e in range(n):
+        by_owner[e] = cluster_for(history, e)
+    for e in range(n):
+        turned = jnp.broadcast_to(places[e], (per_peer, per_peer)).T
+        for c in range(n * room // per_peer):
+            lanes = lax.broadcasted_iota(jnp.int32, (per_peer, per_peer), 1) + c * per_peer
+            place[e * per_peer : (e + 1) * per_peer, c * per_peer : (c + 1) * per_peer] = (
+                jnp.where(turned == lanes.astype(F32), 1.0, 0.0).astype(BF16)
+            )
+
+    def flag_copy(to, slot):
+        return pltpu.make_async_remote_copy(
+            src_ref=flag_mine,
+            dst_ref=flag_all.at[slot],
+            send_sem=flag_send.at[to],
+            recv_sem=flag_recv.at[slot],
+            device_id={"rep": to},
+            device_id_type=MESH,
+        )
+
+    receive(ASK_H, codes, asked_h)
+    full = asked_h[0, :, wide:]
+    for d in range(1, n):
+        full = jnp.maximum(full, asked_h[d, :, wide:])
+    flag_mine[...] = full
+    for off in range(1, reps):
+        flag_copy(rep_peer(off), my_rep).start()
+    flag_all[my_rep] = full
+    for d in range(n):
+        for top in range(0, room, per_peer):
+            size = min(per_peer, room - top)
+            turned = jnp.broadcast_to(asked_h[d, :, top : top + per_peer], (per_peer, per_peer)).T
+            for c in range(height // per_peer):
+                lanes = lax.broadcasted_iota(jnp.int32, (size, per_peer), 1) + c * per_peer
+                pick_h[
+                    d * room + top : d * room + top + size, c * per_peer : (c + 1) * per_peer
+                ] = jnp.where(turned[:size, :] == lanes, 1.0, 0.0).astype(BF16)
+
+    def rows_copy(phase, start, size, to, slot):
+        return pltpu.make_async_remote_copy(
+            src_ref=send_rows.at[to, pl.ds(start, size)],
+            dst_ref=rows_in.at[slot, pl.ds(start, size)],
+            send_sem=send_sem.at[phase, to],
+            recv_sem=recv_sem.at[phase, slot],
+            device_id={"dev": to},
+            device_id_type=MESH,
+        )
+
+    def rows_for(to):
+        rows = pl.ds(pl.multiple_of(to * room, 16), room)
+        values = by_owner[...].reshape(n * cluster, breadth)
+        return jnp.dot(pick_h[rows, :], values, preferred_element_type=F32).astype(BF16)
+
+    def rows_out(off, carry):
+        send_rows[peer(off)] = rows_for(peer(off))
+        rows_copy(H_ONE, 0, early, peer(off), me).start()
+        return carry
+
+    lax.fori_loop(1, n, rows_out, 0)
+    rows_in[me] = rows_for(me)
+
     loads[5].wait()
+    loads[6].wait()
     for i in range(height // tile):
         for j in range(pulled // tile):
             kept = occupancy[i, height // tile + j].astype(F32)
@@ -199,7 +318,7 @@
             part = (edge[rows, cols].astype(F32) * kept).astype(BF16)
             edge[rows, cols] = part
             edge_t[cols, rows] = part.T
-    loads[6].wait()
+    loads[7].wait()
     for i in range(height // tile):
         for j in range(height // tile):
             kept = occupancy[i, j].astype(F32)
@@ -249,13 +368,13 @@
     receive(MOVE_X, send_x, own_x)
     blocks_out(FAR_X, pick_t, own_x, send_far_x, far_x)
     blocks_out(PUSH_ONE, edge_t, own_x, send_one, push_one)
+    for off in range(1, n):
+        rows_copy(H_TWO, early, room - early, peer(off), me).start()
 
     def local_one(rows):
         acc[rows, :] = times(local, rows, own_x)
 
     bands(local_one)
-    receive(MOVE_H, send_h, own_h)
-    blocks_out(FAR_H, pick_t, own_h, send_far_h, far_h)
     receive(FAR_X, send_far_x, far_x)
 
     def edge_one(rows):
@@ -270,8 +389,8 @@
         value = jnp.maximum(value, 0.0).astype(BF16)
         hidden[rows, :] = value
 
-    loads[7].wait()
     loads[8].wait()
+    loads[9].wait()
     bands(first)
     blocks_out(PUSH_TWO, edge_t, hidden, send_two, push_two)
 
@@ -279,14 +398,28 @@
         acc[rows, :] = times(local, rows, hidden)
 
     bands(local_two)
-    receive(FAR_H, send_far_h, far_h)
+    for off in range(1, n):
+        rows_copy(H_ONE, 0, early, peer(off), peer(off)).wait_recv()
+    for off in range(1, n):
+        rows_copy(H_TWO, early, room - early, peer(off), peer(off)).wait_recv()
+
+    def gather_h(rows):
+        far_h[rows, :] = times(place, rows, rows_in).astype(BF16)
+
+    bands(gather_h)
 
     def edge_two(rows):
         acc[rows, :] = acc[rows, :] + times(edge, rows, far_h)
 
     bands(edge_two)
-    loads[9].wait()
     loads[10].wait()
+    loads[11].wait()
+    for off in range(1, reps):
+        flag_copy(rep_peer(off), rep_peer(off)).wait_recv()
+    full = flag_all[0]
+    for r in range(1, reps):
+        full = jnp.maximum(full, flag_all[r])
+    flag_out[0] = jnp.where(jnp.max(full.astype(F32)) > 0.5, 1, 0)
     receive(PUSH_TWO, send_two, push_two)
 
     def second(rows):
@@ -350,9 +483,13 @@
 
     finish(ASK, pulls, asked)
     finish(MOVE_X, send_x, own_x)
-    finish(MOVE_H, send_h, own_h)
     finish(FAR_X, send_far_x, far_x)
-    finish(FAR_H, send_far_h, far_h)
+    finish(ASK_H, codes, asked_h)
+    for off in range(1, n):
+        rows_copy(H_ONE, 0, early, peer(off), me).wait_send()
+        rows_copy(H_TWO, early, room - early, peer(off), me).wait_send()
+    for off in range(1, reps):
+        flag_copy(rep_peer(off), my_rep).wait_send()
     finish(PUSH_ONE, send_one, push_one)
     finish(PUSH_TWO, send_two, push_two)
     for off in range(1, everyone):
@@ -377,7 +514,7 @@
     count = len(values)
     return pl.pallas_call(
         functools.partial(store_kernel, count),
-        out_shape=tuple(jax.ShapeDtypeStruct(v.shape, v.dtype) for v in values),
+        out_shape=tuple(pltpu.HBM(v.shape, v.dtype) for v in values),
         in_specs=[pl.BlockSpec(memory_space=pltpu.VMEM)] * count,
         out_specs=tuple(pl.BlockSpec(memory_space=pl.ANY) for _ in values),
         scratch_shapes=[pltpu.SemaphoreType.DMA((count,))],
@@ -414,20 +551,26 @@
     strip = pltpu.VMEM((part, breadth), BF16)
     weight = pltpu.VMEM((breadth, breadth), BF16)
     nodes = pltpu.VMEM((height, breadth), BF16)
+    room = row_room(per_peer)
+    wide = -(-room // 128) * 128
+    asks = pltpu.VMEM((n, 1, wide + per_peer), jnp.int32)
+    rows = pltpu.VMEM((n, room, breadth), BF16)
     results = pl.pallas_call(
         functools.partial(step_kernel, n, reps, inner),
         out_shape=(
             pltpu.VMEM((height, breadth), BF16),
             pltpu.VMEM((height, breadth), BF16),
             pltpu.VMEM((breadth, breadth), F32),
+            pltpu.SMEM((1,), jnp.int32),
         ),
-        in_specs=[anywhere] * 11,
-        out_specs=(vmem, vmem, vmem),
+        in_specs=[anywhere] * 12,
+        out_specs=(vmem, vmem, vmem, pl.BlockSpec(memory_space=pltpu.SMEM)),
         scratch_shapes=[
             nodes,
             nodes,
             pltpu.SMEM(new_owner.shape, jnp.int32),
             pltpu.VMEM((n, 1, per_peer), jnp.int32),
+            pltpu.VMEM((n, per_peer), jnp.int32),
             pltpu.SMEM(occupancy.shape, jnp.int32),
             weight,
             pltpu.VMEM((1, breadth), F32),
@@ -437,16 +580,20 @@
             pltpu.VMEM((pulled, height), BF16),
             nodes,
             pltpu.VMEM((n, 1, per_peer), jnp.int32),
+            asks,
+            asks,
             pltpu.VMEM((height, pulled), BF16),
             pltpu.VMEM((pulled, height), BF16),
-            moved,
+            pltpu.VMEM((n * room, height), BF16),
+            pltpu.VMEM((pulled, n * room), BF16),
             moved,
             moved,
             moved,
             listed,
+            rows,
             listed,
-            listed,
-            listed,
+            rows,
+            pltpu.VMEM((pulled, breadth), BF16),
             listed,
             listed,
             listed,
@@ -459,13 +606,17 @@
             pltpu.VMEM((n // inner, part, breadth), BF16),
             strip,
             square,
-            pltpu.SemaphoreType.DMA((11,)),
-            pltpu.SemaphoreType.DMA((7, n)),
-            pltpu.SemaphoreType.DMA((7, n)),
+            pltpu.VMEM((1, per_peer), jnp.int32),
+            pltpu.VMEM((reps, 1, per_peer), jnp.int32),
+            pltpu.SemaphoreType.DMA((12,)),
+            pltpu.SemaphoreType.DMA((8, n)),
+            pltpu.SemaphoreType.DMA((8, n)),
             pltpu.SemaphoreType.DMA((2, everyone)),
             pltpu.SemaphoreType.DMA((2, everyone)),
             pltpu.SemaphoreType.DMA((n // inner,)),
             pltpu.SemaphoreType.DMA((n // inner,)),
+            pltpu.SemaphoreType.DMA((reps,)),
+            pltpu.SemaphoreType.DMA((reps,)),
         ],
         compiler_params=pltpu.CompilerParams(
             collective_id=0, has_side_effects=True, vmem_limit_bytes=40 * 1024 * 1024
@@ -478,6 +629,7 @@
                 history,
                 new_owner,
                 pull_rows.reshape(n, 1, per_peer),
+                pull_rows.reshape(n, per_peer),
                 occupancy,
                 adj_local,
                 adj_boundary,
@@ -488,7 +640,15 @@
             )
         )
     )
-    return store(*results)
+    return results
+
+
+def row_room(per_peer):
+    return per_peer * 11 // 8
+
+
+def early_rows(room):
+    return room // 32 * 16
 
 
 def near_width(n):
@@ -499,6 +659,7 @@
     return (
         height % (128 * peers) == 0
         and pulled == 128 * peers
+        and peers * row_room(128) % 128 == 0
         and breadth % (16 * near_width(peers) * reps) == 0
     )
 
@@ -520,7 +681,17 @@
     return (summed, partial_value)
 
 
-def body(
+def body(*args):
+    features, pull_rows = args[0], args[3]
+    peer_count = lax.axis_size("dev")
+    height, breadth = features.shape
+    if not fits(peer_count, height, pull_rows.shape[0], breadth, lax.axis_size("rep")):
+        return plain(*args)
+    *results, full = fused(*args)
+    return lax.cond(full[0] > 0, lambda: store(*plain(*args)), lambda: store(*results))
+
+
+def plain(
     features,
     history,
     new_owner,
@@ -539,20 +710,6 @@
     pulled = pull_rows.shape[0]
     per_peer = pulled // peer_count
     everyone = peer_count * lax.axis_size("rep")
-    if fits(peer_count, height, pulled, breadth, lax.axis_size("rep")):
-        return fused(
-            features,
-            history,
-            new_owner,
-            pull_rows,
-            occupancy,
-            adj_local,
-            adj_boundary,
-            w_first,
-            bias_first,
-            w_second,
-            cotangent,
-        )
     indices = jnp.arange(peer_count, dtype=jnp.int32)
     matches = (new_owner[0][:, None] == indices[None, :]).astype(jnp.int32)
     inverse = jnp.sum(matches * indices[:, None], axis=0)

time: 90.8 us -> 84.9 us (0.935)
  Pallas kernels: 90 us -> 83.5 us
    pallas_call x1, Pallas kernels: 88.9 us -> 82.4 us  [fused(): pl.pallas_call(functools.partial(step_kernel, n, reps, inner), out_shape=...]
where the time goes in v2:
time: 84.9 us; the launch traced here: 84.7 us
  Pallas kernels  83.5 us (98%)
  between operations  0.94 us (1%)
    pallas_call x1, Pallas kernels, fused(): pl.pallas_call(functools.partial(step_kernel, n, reps, inner), out_shape=...  82.4 us

profile of v2, /device:TPU:0, one launch (start us, length us, event | category | flops | bytes accessed | tf_op | source)
XLA Modules:
  0.0 84.7 jit_solution(11706514359166856848)
XLA Ops:
  0.6 0.0 copy-start.3
  0.6 0.0 copy-start.4
  0.7 0.0 copy-start.5
  0.7 0.0 copy-start.6
  0.7 0.0 copy-start.7
  0.7 0.0 copy-start.8
  0.7 0.0 copy-start.9
  0.7 82.4 %shard_map.136 = (bf16[1024,256]{1,0:T(8,128)(2,1)S(1)}, bf16[1024,256]{1,0:T(8,128)(2,1)S(1)}, f32[256,256]{1,0:T(8,128)S(1)}, s32[1]{0:T(128)S(4)}) custom-call(bf16[1024,256]{1,0:T(8,128)(2,1)} %features_hbm.1, bf16[1024,256]{1,0:T(8,128)(2,1)} %history_hbm.1, s32[1,8]{1,0:T(1,128)} %new_owner_hbm.1, s32[8,1,128]{2,1,0:T(1,128)} %bitcast.21.pulls_hbm, ...), custom_call_target="tpu_custom_call" | custom-call | tf_op jit(solution)/shard_map/pallas_call | solution.py:558
  83.2 0.0 copy-done.3
  83.2 0.0 copy-done.4
  83.2 0.0 copy-done.5
  83.2 0.0 copy-done.6
  83.2 0.0 copy-done.7
  83.2 0.0 copy-done.8
  83.2 0.0 copy-done.9
  83.2 1.3 %conditional.1 = ((bf16[1024,256]{1,0:T(8,128)(2,1)}, bf16[1024,256]{1,0:T(8,128)(2,1)}, f32[256,256]{1,0:T(8,128)})) conditional(s32[]{:T(128)} %bitcast.24, (bf16[1024,256]{1,0:T(8,128)(2,1)S(1)}, bf16[1024,256]{1,0:T(8,128)(2,1)S(1)}, f32[256,256]{1,0:T(8,128)S(1)}) %tuple.13, (s32[8,16]{1,0:T(8,128)S(1)}, bf16[1024,1024]{1,0:T(8,128)(2,1)}, ...), branch_computations={%region_0.0_spmd, %region_1.0_spmd} | conditional | flops 4706077696 | bytes 95291976 | solution.py:691
  83.2 1.1 %branch_0_fun.1 = (bf16[1024,256]{1,0:T(8,128)(2,1)}, bf16[1024,256]{1,0:T(8,128)(2,1)}, f32[256,256]{1,0:T(8,128)}) custom-call(bf16[1024,256]{1,0:T(8,128)(2,1)S(1)} %get-tuple-element.28.refs_0_, bf16[1024,256]{1,0:T(8,128)(2,1)S(1)} %get-tuple-element.29.refs_1_, f32[256,256]{1,0:T(8,128)S(1)} %get-tuple-element.30.refs_2_), custom_call_target="tpu_custom_call" | custom-call | tf_op jit(solution)/shard_map/cond/branch_0_fun/pallas_call | solution.py:515
Async XLA Ops:
  0.6 82.5 %copy-start.3 = (bf16[1024,256]{1,0:T(8,128)(2,1)S(1)}, bf16[1024,256]{1,0:T(8,128)(2,1)}, u32[]{:S(2)}) copy-start(bf16[1024,256]{1,0:T(8,128)(2,1)} %features_hbm.1) | copy-start | bytes 1572868
  0.6 82.5 %copy-start.4 = (bf16[1024,256]{1,0:T(8,128)(2,1)S(1)}, bf16[1024,256]{1,0:T(8,128)(2,1)}, u32[]{:S(2)}) copy-start(bf16[1024,256]{1,0:T(8,128)(2,1)} %history_hbm.1) | copy-start | bytes 1572868
  0.7 82.5 %copy-start.5 = (bf16[256,256]{1,0:T(8,128)(2,1)S(1)}, bf16[256,256]{1,0:T(8,128)(2,1)}, u32[]{:S(2)}) copy-start(bf16[256,256]{1,0:T(8,128)(2,1)} %w_second_hbm.1) | copy-start | bytes 393220
  0.7 82.5 %copy-start.6 = (bf16[256,256]{1,0:T(8,128)(2,1)S(1)}, bf16[256,256]{1,0:T(8,128)(2,1)}, u32[]{:S(2)}) copy-start(bf16[256,256]{1,0:T(8,128)(2,1)} %w_first_hbm.1) | copy-start | bytes 393220
  0.7 82.5 %copy-start.7 = (s32[8,16]{1,0:T(8,128)S(1)}, s32[8,16]{1,0:T(8,128)}, u32[]{:S(2)}) copy-start(s32[8,16]{1,0:T(8,128)} %occupancy_hbm.1) | copy-start | bytes 1540
  0.7 82.5 %copy-start.8 = (f32[256]{0:T(256)S(1)}, f32[256]{0:T(256)}, u32[]{:S(2)}) copy-start(f32[256]{0:T(256)} %param.21) | copy-start | bytes 3076
  0.7 82.5 %copy-start.9 = (s32[1,8]{1,0:T(1,128)S(1)}, s32[1,8]{1,0:T(1,128)}, u32[]{:S(2)}) copy-start(s32[1,8]{1,0:T(1,128)} %new_owner_hbm.1) | copy-start | bytes 100

commit v3 on v2

--- a/solution.py
+++ b/solution.py
@@ -10,7 +10,7 @@
 MESH = pl.DeviceIdType.MESH
 F32 = jnp.float32
 BF16 = jnp.bfloat16
-ASK, ASK_H, MOVE_X, FAR_X, H_ONE, H_TWO, PUSH_ONE, PUSH_TWO = range(8)
+ASK, ASK_H, MOVE_X, FAR_X, H_ONE, H_TWO, NEAR_X, PUSH_ONE, PUSH_TWO = range(9)
 
 
 def step_kernel(
@@ -53,12 +53,17 @@
     pick_t,
     pick_h,
     place,
+    pick_n,
+    place_x,
+    seat_x,
     send_x,
     by_owner,
     own_x,
     send_far_x,
     send_rows,
+    send_near,
     far_x,
+    mix,
     rows_in,
     far_h,
     send_one,
@@ -95,7 +100,18 @@
     band = min(256, height)
     room = send_rows.shape[1]
     early = early_rows(room)
-    wide = codes.shape[2] - per_peer
+    wide = codes.shape[2] - 3 * per_peer
+    half = n // 2
+    depth = mix.shape[1]
+    cross = cross_rows(per_peer)
+    home = lax.rem(me, half)
+    side = me // half
+
+    def beside(off):
+        return side * half + lax.rem(home + off, half)
+
+    def across(off):
+        return (1 - side) * half + lax.rem(home + off, half)
 
     def peer(off):
         return lax.rem(me + off, n)
@@ -123,13 +139,13 @@
     barrier = pltpu.get_barrier_semaphore()
     for off in range(1, n):
         pl.semaphore_signal(barrier, inc=1, device_id={"dev": peer(off)}, device_id_type=MESH)
-    for side in range(inner):
+    for lane in range(inner):
         for off in range(1, reps):
             pl.semaphore_signal(
                 barrier,
                 inc=1,
                 device_id={
-                    "dev": line * inner + lax.rem(me + side, inner),
+                    "dev": line * inner + lax.rem(me + lane, inner),
                     "rep": rep_peer(off),
                 },
                 device_id_type=MESH,
@@ -209,7 +225,47 @@
         before = jnp.full((n, per_peer), -1.0, F32)
         over = jnp.zeros((n, per_peer), F32)
         table = jnp.zeros((2 * n, wide), F32)
+        lanes = seats[:per_peer]
+        away = (origin // half != side).astype(F32)
+        nearby = 1.0 - away
+        spot_s = lax.rem(origin, half) + half
+        behind = jnp.full((n, per_peer), -1.0, F32)
+        table_n = jnp.zeros((2 * n, per_peer), F32)
         places = []
+        for e in range(n):
+            remote = jnp.where(e // half != side, 1.0, 0.0)
+            ahead = prefix[e * n : (e + 1) * n, :]
+            rank = jnp.sum(ahead * away, axis=0, keepdims=True) - 1.0
+            gone = held[e] * away
+            stays = held[e] * nearby * remote
+            seat = stays * (ahead + behind)
+            behind = behind + remote * totals[e * n : (e + 1) * n, :]
+            over = jnp.maximum(over, seat + float(room - depth))
+            over = jnp.maximum(over, remote * gone * rank + float(room - cross))
+            seat_x[e] = jnp.sum(
+                seat
+                + stays * (spot_s * depth).astype(F32)
+                + gone * (rank + float(e % half * depth)),
+                axis=0,
+                keepdims=True,
+            )
+            taken = jnp.where(lanes == rank, 1.0, 0.0).astype(BF16)
+            entry = jnp.concatenate([gone * origin.astype(F32), gone * within[e]], axis=0)
+            listed = lax.dot_general(
+                entry.astype(BF16), taken, (((1,), (1,)), ((), ())), preferred_element_type=F32
+            )
+            listed = jnp.sum(
+                listed[:n, :] * float(cluster) + listed[n:, :], axis=0, keepdims=True
+            ).astype(jnp.int32)
+            codes[e, :, wide + per_peer : wide + 2 * per_peer] = jnp.where(
+                e // half != side, listed, lists[e : e + 1, :]
+            )
+            mine = jnp.sum(seat, axis=0, keepdims=True)
+            taken = jnp.where(lanes == mine, 1.0, 0.0).astype(BF16)
+            entry = jnp.concatenate([stays * float(e), stays * within[e]], axis=0)
+            table_n = table_n + lax.dot_general(
+                entry.astype(BF16), taken, (((1,), (1,)), ((), ())), preferred_element_type=F32
+            )
         for e in range(n):
             seat = held[e] * (prefix[e * n : (e + 1) * n, :] + before)
             before = before + totals[e * n : (e + 1) * n, :]
@@ -225,9 +281,11 @@
             )
         found = (table[:n, :] * float(cluster) + table[n:, :]).astype(jnp.int32)
         full = jnp.where(jnp.max(over, axis=0, keepdims=True) >= float(room), 1, 0)
+        found_n = (table_n[:n, :] * float(cluster) + table_n[n:, :]).astype(jnp.int32)
         for d in range(n):
             codes[d, :, :wide] = found[d : d + 1, :]
-            codes[d, :, wide:] = full
+            codes[d, :, wide : wide + per_peer] = full
+            codes[d, :, wide + 2 * per_peer :] = found_n[d : d + 1, :]
         return places
 
     loads[2].wait()
@@ -237,6 +295,7 @@
     for off in range(1, n):
         send_x[peer(off)] = cluster_for(features, peer(off))
     own_x[me] = cluster_for(features, me)
+    send_x[me] = own_x[me]
     loads[3].wait()
     pl.semaphore_wait(barrier, n - 1 + inner * (reps - 1))
     for off in range(1, n):
@@ -269,9 +328,9 @@
         )
 
     receive(ASK_H, codes, asked_h)
-    full = asked_h[0, :, wide:]
+    full = asked_h[0, :, wide : wide + per_peer]
     for d in range(1, n):
-        full = jnp.maximum(full, asked_h[d, :, wide:])
+        full = jnp.maximum(full, asked_h[d, :, wide : wide + per_peer])
     flag_mine[...] = full
     for off in range(1, reps):
         flag_copy(rep_peer(off), my_rep).start()
@@ -308,6 +367,44 @@
 
     lax.fori_loop(1, n, rows_out, 0)
     rows_in[me] = rows_for(me)
+
+    for o in range(half):
+        turned = jnp.broadcast_to(
+            asked_h[beside(o), :, wide + 2 * per_peer :], (per_peer, per_peer)
+        ).T
+        for c in range(height // per_peer):
+            lanes = lax.broadcasted_iota(jnp.int32, (depth, per_peer), 1) + c * per_peer
+            pick_n[o * depth : (o + 1) * depth, c * per_peer : (c + 1) * per_peer] = jnp.where(
+                turned[:depth, :] == lanes, 1.0, 0.0
+            ).astype(BF16)
+
+    def near_rows(to, at, slot):
+        return pltpu.make_async_remote_copy(
+            src_ref=send_near.at[at],
+            dst_ref=mix.at[half + slot],
+            send_sem=send_sem.at[NEAR_X, to],
+            recv_sem=recv_sem.at[NEAR_X, side * half + slot],
+            device_id={"dev": to},
+            device_id_type=MESH,
+        )
+
+    moved_rows = jnp.dot(
+        pick_n[...],
+        send_x[...].reshape(n * cluster, breadth),
+        preferred_element_type=F32,
+    ).astype(BF16)
+    mix[half + home] = moved_rows[:depth, :]
+    for o in range(1, half):
+        send_near[o] = moved_rows[o * depth : (o + 1) * depth, :]
+        near_rows(beside(o), o, home).start()
+    for o in range(half):
+        mix[o, cross:, :] = jnp.zeros((depth - cross, breadth), BF16)
+        turned = jnp.broadcast_to(seat_x[across(o)], (per_peer, per_peer)).T
+        for c in range(n * depth // per_peer):
+            lanes = lax.broadcasted_iota(jnp.int32, (per_peer, per_peer), 1) + c * per_peer
+            place_x[o * per_peer : (o + 1) * per_peer, c * per_peer : (c + 1) * per_peer] = (
+                jnp.where(turned == lanes.astype(F32), 1.0, 0.0).astype(BF16)
+            )
 
     loads[5].wait()
     loads[6].wait()
@@ -332,7 +429,8 @@
         pick[:, d * per_peer : (d + 1) * per_peer] = jnp.where(rows == wanted, 1.0, 0.0).astype(
             BF16
         )
-        turned = jnp.broadcast_to(wanted, (per_peer, per_peer)).T
+        listed = asked_h[d, :, wide + per_peer : wide + 2 * per_peer]
+        turned = jnp.broadcast_to(listed, (per_peer, per_peer)).T
         lanes = lax.broadcasted_iota(jnp.int32, (per_peer, per_peer), 1)
         for c in range(height // per_peer):
             pick_t[d * per_peer : (d + 1) * per_peer, c * per_peer : (c + 1) * per_peer] = (
@@ -366,7 +464,47 @@
         return jnp.dot(left[rows, :], values, preferred_element_type=F32)
 
     receive(MOVE_X, send_x, own_x)
-    blocks_out(FAR_X, pick_t, own_x, send_far_x, far_x)
+
+    def cross_copy(to, slot):
+        return pltpu.make_async_remote_copy(
+            src_ref=send_far_x.at[to, pl.ds(0, cross)],
+            dst_ref=mix.at[slot, pl.ds(0, cross)],
+            send_sem=send_sem.at[FAR_X, to],
+            recv_sem=recv_sem.at[FAR_X, (1 - side) * half + slot],
+            device_id={"dev": to},
+            device_id_type=MESH,
+        )
+
+    def cross_sent(to, slot):
+        return pltpu.make_async_remote_copy(
+            src_ref=send_far_x.at[to, pl.ds(0, cross)],
+            dst_ref=mix.at[slot, pl.ds(0, cross)],
+            send_sem=send_sem.at[FAR_X, to],
+            recv_sem=recv_sem.at[FAR_X, side * half + slot],
+            device_id={"dev": to},
+            device_id_type=MESH,
+        )
+
+    def far_block(to):
+        rows = pl.ds(pl.multiple_of(to * per_peer, per_peer), per_peer)
+        values = own_x[...].reshape(height, breadth)
+        return jnp.dot(pick_t[rows, :], values, preferred_element_type=F32).astype(BF16)
+
+    def far_across(o, carry):
+        to = across(o)
+        send_far_x[to] = far_block(to)
+        cross_sent(to, home).start()
+        return carry
+
+    def far_beside(o, carry):
+        to = beside(o)
+        send_far_x[to] = far_block(to)
+        outgoing(FAR_X, send_far_x, far_x, to, me).start()
+        return carry
+
+    lax.fori_loop(0, half, far_across, 0)
+    lax.fori_loop(1, half, far_beside, 0)
+    far_x[me] = far_block(me)
     blocks_out(PUSH_ONE, edge_t, own_x, send_one, push_one)
     for off in range(1, n):
         rows_copy(H_TWO, early, room - early, peer(off), me).start()
@@ -375,7 +513,18 @@
         acc[rows, :] = times(local, rows, own_x)
 
     bands(local_one)
-    receive(FAR_X, send_far_x, far_x)
+    for o in range(1, half):
+        other = beside(o)
+        outgoing(FAR_X, send_far_x, far_x, other, other).wait_recv()
+        near_rows(other, o, lax.rem(home + o, half)).wait_recv()
+    for o in range(half):
+        cross_copy(across(o), lax.rem(home + o, half)).wait_recv()
+    for o in range(half):
+        far_x[across(o)] = jnp.dot(
+            place_x[o * per_peer : (o + 1) * per_peer, :],
+            mix[...].reshape(n * depth, breadth),
+            preferred_element_type=F32,
+        ).astype(BF16)
 
     def edge_one(rows):
         acc[rows, :] = acc[rows, :] + times(edge, rows, far_x)
@@ -483,7 +632,11 @@
 
     finish(ASK, pulls, asked)
     finish(MOVE_X, send_x, own_x)
-    finish(FAR_X, send_far_x, far_x)
+    for o in range(half):
+        cross_sent(across(o), home).wait_send()
+    for o in range(1, half):
+        outgoing(FAR_X, send_far_x, far_x, beside(o), me).wait_send()
+        near_rows(beside(o), o, home).wait_send()
     finish(ASK_H, codes, asked_h)
     for off in range(1, n):
         rows_copy(H_ONE, 0, early, peer(off), me).wait_send()
@@ -553,7 +706,9 @@
     nodes = pltpu.VMEM((height, breadth), BF16)
     room = row_room(per_peer)
     wide = -(-room // 128) * 128
-    asks = pltpu.VMEM((n, 1, wide + per_peer), jnp.int32)
+    asks = pltpu.VMEM((n, 1, wide + 3 * per_peer), jnp.int32)
+    half = n // 2
+    depth = near_rows_room(per_peer)
     rows = pltpu.VMEM((n, room, breadth), BF16)
     results = pl.pallas_call(
         functools.partial(step_kernel, n, reps, inner),
@@ -586,12 +741,17 @@
             pltpu.VMEM((pulled, height), BF16),
             pltpu.VMEM((n * room, height), BF16),
             pltpu.VMEM((pulled, n * room), BF16),
+            pltpu.VMEM((half * depth, height), BF16),
+            pltpu.VMEM((half * per_peer, n * depth), BF16),
+            pltpu.VMEM((n, 1, per_peer), F32),
             moved,
             moved,
             moved,
             listed,
             rows,
+            pltpu.VMEM((half, depth, breadth), BF16),
             listed,
+            pltpu.VMEM((n, depth, breadth), BF16),
             rows,
             pltpu.VMEM((pulled, breadth), BF16),
             listed,
@@ -609,8 +769,8 @@
             pltpu.VMEM((1, per_peer), jnp.int32),
             pltpu.VMEM((reps, 1, per_peer), jnp.int32),
             pltpu.SemaphoreType.DMA((12,)),
-            pltpu.SemaphoreType.DMA((8, n)),
-            pltpu.SemaphoreType.DMA((8, n)),
+            pltpu.SemaphoreType.DMA((9, n)),
+            pltpu.SemaphoreType.DMA((9, n)),
             pltpu.SemaphoreType.DMA((2, everyone)),
             pltpu.SemaphoreType.DMA((2, everyone)),
             pltpu.SemaphoreType.DMA((n // inner,)),
@@ -647,6 +807,14 @@
     return per_peer * 11 // 8
 
 
+def near_rows_room(per_peer):
+    return per_peer * 7 // 8
+
+
+def cross_rows(per_peer):
+    return per_peer * 3 // 4
+
+
 def early_rows(room):
     return room // 32 * 16
 
@@ -659,7 +827,9 @@
     return (
         height % (128 * peers) == 0
         and pulled == 128 * peers
+        and peers % 2 == 0
         and peers * row_room(128) % 128 == 0
+        and peers * near_rows_room(128) % 128 == 0
         and breadth % (16 * near_width(peers) * reps) == 0
     )
 

time: 84.9 us -> 82.4 us (0.971)
  Pallas kernels: 83.5 us -> 81 us
    pallas_call x1, Pallas kernels: 82.4 us -> 80 us  [fused(): pl.pallas_call(functools.partial(step_kernel, n, reps, inner), out_shape=...]
where the time goes in v3:
time: 82.4 us; the launch traced here: 82.3 us
  Pallas kernels  81 us (98%)
  between operations  0.94 us (1%)
    pallas_call x1, Pallas kernels, fused(): pl.pallas_call(functools.partial(step_kernel, n, reps, inner), out_shape=...  80 us

profile of v3, /device:TPU:0, one launch (start us, length us, event | category | flops | bytes accessed | tf_op | source)
XLA Modules:
  0.0 82.3 jit_solution(201813783000709769)
XLA Ops:
  0.6 0.0 copy-start.3
  0.6 0.0 copy-start.4
  0.7 0.0 copy-start.5
  0.7 0.0 copy-start.6
  0.7 0.0 copy-start.7
  0.7 0.0 copy-start.8
  0.7 0.0 copy-start.9
  0.7 80.0 %shard_map.136 = (bf16[1024,256]{1,0:T(8,128)(2,1)S(1)}, bf16[1024,256]{1,0:T(8,128)(2,1)S(1)}, f32[256,256]{1,0:T(8,128)S(1)}, s32[1]{0:T(128)S(4)}) custom-call(bf16[1024,256]{1,0:T(8,128)(2,1)} %features_hbm.1, bf16[1024,256]{1,0:T(8,128)(2,1)} %history_hbm.1, s32[1,8]{1,0:T(1,128)} %new_owner_hbm.1, s32[8,1,128]{2,1,0:T(1,128)} %bitcast.21.pulls_hbm, ...), custom_call_target="tpu_custom_call" | custom-call | tf_op jit(solution)/shard_map/pallas_call | solution.py:713
  80.7 0.0 copy-done.3
  80.7 0.0 copy-done.4
  80.7 0.0 copy-done.5
  80.7 0.0 copy-done.6
  80.7 0.0 copy-done.7
  80.7 0.0 copy-done.8
  80.7 0.0 copy-done.9
  80.8 1.3 %conditional.1 = ((bf16[1024,256]{1,0:T(8,128)(2,1)}, bf16[1024,256]{1,0:T(8,128)(2,1)}, f32[256,256]{1,0:T(8,128)})) conditional(s32[]{:T(128)} %bitcast.24, (bf16[1024,256]{1,0:T(8,128)(2,1)S(1)}, bf16[1024,256]{1,0:T(8,128)(2,1)S(1)}, f32[256,256]{1,0:T(8,128)S(1)}) %tuple.13, (s32[8,16]{1,0:T(8,128)S(1)}, bf16[1024,1024]{1,0:T(8,128)(2,1)}, ...), branch_computations={%region_0.0_spmd, %region_1.0_spmd} | conditional | flops 4706077696 | bytes 95291976 | solution.py:861
  80.8 1.1 %branch_0_fun.1 = (bf16[1024,256]{1,0:T(8,128)(2,1)}, bf16[1024,256]{1,0:T(8,128)(2,1)}, f32[256,256]{1,0:T(8,128)}) custom-call(bf16[1024,256]{1,0:T(8,128)(2,1)S(1)} %get-tuple-element.28.refs_0_, bf16[1024,256]{1,0:T(8,128)(2,1)S(1)} %get-tuple-element.29.refs_1_, f32[256,256]{1,0:T(8,128)S(1)} %get-tuple-element.30.refs_2_), custom_call_target="tpu_custom_call" | custom-call | tf_op jit(solution)/shard_map/cond/branch_0_fun/pallas_call | solution.py:668
Async XLA Ops:
  0.6 80.1 %copy-start.3 = (bf16[1024,256]{1,0:T(8,128)(2,1)S(1)}, bf16[1024,256]{1,0:T(8,128)(2,1)}, u32[]{:S(2)}) copy-start(bf16[1024,256]{1,0:T(8,128)(2,1)} %features_hbm.1) | copy-start | bytes 1572868
  0.6 80.1 %copy-start.4 = (bf16[1024,256]{1,0:T(8,128)(2,1)S(1)}, bf16[1024,256]{1,0:T(8,128)(2,1)}, u32[]{:S(2)}) copy-start(bf16[1024,256]{1,0:T(8,128)(2,1)} %history_hbm.1) | copy-start | bytes 1572868
  0.7 80.1 %copy-start.5 = (bf16[256,256]{1,0:T(8,128)(2,1)S(1)}, bf16[256,256]{1,0:T(8,128)(2,1)}, u32[]{:S(2)}) copy-start(bf16[256,256]{1,0:T(8,128)(2,1)} %w_second_hbm.1) | copy-start | bytes 393220
  0.7 80.1 %copy-start.6 = (bf16[256,256]{1,0:T(8,128)(2,1)S(1)}, bf16[256,256]{1,0:T(8,128)(2,1)}, u32[]{:S(2)}) copy-start(bf16[256,256]{1,0:T(8,128)(2,1)} %w_first_hbm.1) | copy-start | bytes 393220
  0.7 80.1 %copy-start.7 = (s32[8,16]{1,0:T(8,128)S(1)}, s32[8,16]{1,0:T(8,128)}, u32[]{:S(2)}) copy-start(s32[8,16]{1,0:T(8,128)} %occupancy_hbm.1) | copy-start | bytes 1540
  0.7 80.1 %copy-start.8 = (f32[256]{0:T(256)S(1)}, f32[256]{0:T(256)}, u32[]{:S(2)}) copy-start(f32[256]{0:T(256)} %param.21) | copy-start | bytes 3076
  0.7 80.1 %copy-start.9 = (s32[1,8]{1,0:T(1,128)S(1)}, s32[1,8]{1,0:T(1,128)}, u32[]{:S(2)}) copy-start(s32[1,8]{1,0:T(1,128)} %new_owner_hbm.1) | copy-start | bytes 100

commit v4 on v3

--- a/solution.py
+++ b/solution.py
@@ -10,7 +10,7 @@
 MESH = pl.DeviceIdType.MESH
 F32 = jnp.float32
 BF16 = jnp.bfloat16
-ASK, ASK_H, MOVE_X, FAR_X, H_ONE, H_TWO, NEAR_X, PUSH_ONE, PUSH_TWO = range(9)
+ASK, ASK_H, MOVE_X, FAR_X, H_ONE, H_TWO, NEAR_X, FAR_B, PUSH_ONE, PUSH_TWO = range(10)
 
 
 def step_kernel(
@@ -185,23 +185,36 @@
         return pltpu.make_async_remote_copy(
             src_ref=src.at[to],
             dst_ref=dst.at[slot],
-            send_sem=send_sem.at[phase, to],
-            recv_sem=recv_sem.at[phase, slot],
+            send_sem=send_sem.at[phase],
+            recv_sem=recv_sem.at[phase],
             device_id={"dev": to},
             device_id_type=MESH,
         )
 
+    def bulk(piece, sent, arrived):
+        return pltpu.make_async_remote_copy(
+            src_ref=piece,
+            dst_ref=piece,
+            send_sem=sent,
+            recv_sem=arrived,
+            device_id={"dev": peer(1)},
+            device_id_type=MESH,
+        )
+
+    def arrived(phase, piece):
+        bulk(piece, send_sem.at[phase], recv_sem.at[phase]).wait_recv()
+
+    def left(phase, piece):
+        bulk(piece, send_sem.at[phase], recv_sem.at[phase]).wait_send()
+
     def send(phase, src, dst, off):
         outgoing(phase, src, dst, peer(off), me).start()
 
     def receive(phase, src, dst):
-        for off in range(1, n):
-            other = peer(off)
-            outgoing(phase, src, dst, other, other).wait_recv()
+        arrived(phase, dst.at[pl.ds(0, n - 1)])
 
     def finish(phase, src, dst):
-        for off in range(1, n):
-            outgoing(phase, src, dst, peer(off), me).wait_send()
+        left(phase, src.at[pl.ds(0, n - 1)])
 
     def slots():
         upper = jnp.where(
@@ -321,8 +334,8 @@
         return pltpu.make_async_remote_copy(
             src_ref=flag_mine,
             dst_ref=flag_all.at[slot],
-            send_sem=flag_send.at[to],
-            recv_sem=flag_recv.at[slot],
+            send_sem=flag_send,
+            recv_sem=flag_recv,
             device_id={"rep": to},
             device_id_type=MESH,
         )
@@ -349,8 +362,8 @@
         return pltpu.make_async_remote_copy(
             src_ref=send_rows.at[to, pl.ds(start, size)],
             dst_ref=rows_in.at[slot, pl.ds(start, size)],
-            send_sem=send_sem.at[phase, to],
-            recv_sem=recv_sem.at[phase, slot],
+            send_sem=send_sem.at[phase],
+            recv_sem=recv_sem.at[phase],
             device_id={"dev": to},
             device_id_type=MESH,
         )
@@ -382,8 +395,8 @@
         return pltpu.make_async_remote_copy(
             src_ref=send_near.at[at],
             dst_ref=mix.at[half + slot],
-            send_sem=send_sem.at[NEAR_X, to],
-            recv_sem=recv_sem.at[NEAR_X, side * half + slot],
+            send_sem=send_sem.at[NEAR_X],
+            recv_sem=recv_sem.at[NEAR_X],
             device_id={"dev": to},
             device_id_type=MESH,
         )
@@ -465,22 +478,12 @@
 
     receive(MOVE_X, send_x, own_x)
 
-    def cross_copy(to, slot):
-        return pltpu.make_async_remote_copy(
-            src_ref=send_far_x.at[to, pl.ds(0, cross)],
-            dst_ref=mix.at[slot, pl.ds(0, cross)],
-            send_sem=send_sem.at[FAR_X, to],
-            recv_sem=recv_sem.at[FAR_X, (1 - side) * half + slot],
-            device_id={"dev": to},
-            device_id_type=MESH,
-        )
-
     def cross_sent(to, slot):
         return pltpu.make_async_remote_copy(
             src_ref=send_far_x.at[to, pl.ds(0, cross)],
             dst_ref=mix.at[slot, pl.ds(0, cross)],
-            send_sem=send_sem.at[FAR_X, to],
-            recv_sem=recv_sem.at[FAR_X, side * half + slot],
+            send_sem=send_sem.at[FAR_X],
+            recv_sem=recv_sem.at[FAR_X],
             device_id={"dev": to},
             device_id_type=MESH,
         )
@@ -499,7 +502,7 @@
     def far_beside(o, carry):
         to = beside(o)
         send_far_x[to] = far_block(to)
-        outgoing(FAR_X, send_far_x, far_x, to, me).start()
+        outgoing(FAR_B, send_far_x, far_x, to, me).start()
         return carry
 
     lax.fori_loop(0, half, far_across, 0)
@@ -513,12 +516,9 @@
         acc[rows, :] = times(local, rows, own_x)
 
     bands(local_one)
-    for o in range(1, half):
-        other = beside(o)
-        outgoing(FAR_X, send_far_x, far_x, other, other).wait_recv()
-        near_rows(other, o, lax.rem(home + o, half)).wait_recv()
-    for o in range(half):
-        cross_copy(across(o), lax.rem(home + o, half)).wait_recv()
+    arrived(FAR_B, far_x.at[pl.ds(0, half - 1)])
+    arrived(NEAR_X, mix.at[pl.ds(0, half - 1)])
+    arrived(FAR_X, mix.at[pl.ds(0, half), pl.ds(0, cross)])
     for o in range(half):
         far_x[across(o)] = jnp.dot(
             place_x[o * per_peer : (o + 1) * per_peer, :],
@@ -547,10 +547,8 @@
         acc[rows, :] = times(local, rows, hidden)
 
     bands(local_two)
-    for off in range(1, n):
-        rows_copy(H_ONE, 0, early, peer(off), peer(off)).wait_recv()
-    for off in range(1, n):
-        rows_copy(H_TWO, early, room - early, peer(off), peer(off)).wait_recv()
+    arrived(H_ONE, rows_in.at[pl.ds(0, n - 1), pl.ds(0, early)])
+    arrived(H_TWO, rows_in.at[pl.ds(0, n - 1), pl.ds(early, room - early)])
 
     def gather_h(rows):
         far_h[rows, :] = times(place, rows, rows_in).astype(BF16)
@@ -563,8 +561,8 @@
     bands(edge_two)
     loads[10].wait()
     loads[11].wait()
-    for off in range(1, reps):
-        flag_copy(rep_peer(off), rep_peer(off)).wait_recv()
+    if reps > 1:
+        bulk(flag_all.at[pl.ds(0, reps - 1)], flag_send, flag_recv).wait_recv()
     full = flag_all[0]
     for r in range(1, reps):
         full = jnp.maximum(full, flag_all[r])
@@ -584,8 +582,8 @@
         return pltpu.make_async_remote_copy(
             src_ref=src,
             dst_ref=dst.at[slot],
-            send_sem=near_send.at[phase, to],
-            recv_sem=near_recv.at[phase, slot],
+            send_sem=near_send.at[phase],
+            recv_sem=near_recv.at[phase],
             device_id=near_id(to),
             device_id_type=MESH,
         )
@@ -594,8 +592,8 @@
         return pltpu.make_async_remote_copy(
             src_ref=strip_mine,
             dst_ref=strip_far.at[slot],
-            send_sem=far_send.at[to],
-            recv_sem=far_recv.at[slot],
+            send_sem=far_send,
+            recv_sem=far_recv,
             device_id=far_id(to),
             device_id_type=MESH,
         )
@@ -610,15 +608,14 @@
 
     bands(last)
     total = grad_mine[spot].astype(F32)
+    bulk(grad_near.at[pl.ds(0, everyone - 1)], near_send.at[0], near_recv.at[0]).wait_recv()
     for off in range(1, everyone):
-        near_copy(0, grad_mine.at[near(off)], grad_near, near(off), near(off)).wait_recv()
         total = total + grad_near[near(off)].astype(F32)
     strip_mine[...] = total.astype(BF16)
     for off in range(1, outer):
         far_copy(far(off), line).start()
     strip_far[line] = strip_mine[...]
-    for off in range(1, outer):
-        far_copy(far(off), far(off)).wait_recv()
+    bulk(strip_far.at[pl.ds(0, outer - 1)], far_send, far_recv).wait_recv()
     total = strip_far[0].astype(F32)
     for z in range(1, outer):
         total = total + strip_far[z].astype(F32)
@@ -626,30 +623,24 @@
     for off in range(1, everyone):
         near_copy(1, total_mine, grad_all, near(off), spot).start()
     grad_all[spot] = total_mine[...]
-    for off in range(1, everyone):
-        near_copy(1, total_mine, grad_all, near(off), near(off)).wait_recv()
+    bulk(grad_all.at[pl.ds(0, everyone - 1)], near_send.at[1], near_recv.at[1]).wait_recv()
     grad_out[...] = grad_all[...].astype(F32).reshape(grad_out.shape)
 
     finish(ASK, pulls, asked)
     finish(MOVE_X, send_x, own_x)
-    for o in range(half):
-        cross_sent(across(o), home).wait_send()
-    for o in range(1, half):
-        outgoing(FAR_X, send_far_x, far_x, beside(o), me).wait_send()
-        near_rows(beside(o), o, home).wait_send()
+    left(FAR_X, send_far_x.at[pl.ds(0, half), pl.ds(0, cross)])
+    left(FAR_B, send_far_x.at[pl.ds(0, half - 1)])
+    left(NEAR_X, send_near.at[pl.ds(0, half - 1)])
     finish(ASK_H, codes, asked_h)
-    for off in range(1, n):
-        rows_copy(H_ONE, 0, early, peer(off), me).wait_send()
-        rows_copy(H_TWO, early, room - early, peer(off), me).wait_send()
-    for off in range(1, reps):
-        flag_copy(rep_peer(off), my_rep).wait_send()
+    left(H_ONE, send_rows.at[pl.ds(0, n - 1), pl.ds(0, early)])
+    left(H_TWO, send_rows.at[pl.ds(0, n - 1), pl.ds(early, room - early)])
+    if reps > 1:
+        bulk(flag_all.at[pl.ds(0, reps - 1)], flag_send, flag_recv).wait_send()
     finish(PUSH_ONE, send_one, push_one)
     finish(PUSH_TWO, send_two, push_two)
-    for off in range(1, everyone):
-        near_copy(0, grad_mine.at[near(off)], grad_near, near(off), spot).wait_send()
-        near_copy(1, total_mine, grad_all, near(off), spot).wait_send()
-    for off in range(1, outer):
-        far_copy(far(off), line).wait_send()
+    bulk(grad_near.at[pl.ds(0, everyone - 1)], near_send.at[0], near_recv.at[0]).wait_send()
+    bulk(grad_all.at[pl.ds(0, everyone - 1)], near_send.at[1], near_recv.at[1]).wait_send()
+    bulk(strip_far.at[pl.ds(0, outer - 1)], far_send, far_recv).wait_send()
 
 
 def store_kernel(count, *refs):
@@ -769,14 +760,14 @@
             pltpu.VMEM((1, per_peer), jnp.int32),
             pltpu.VMEM((reps, 1, per_peer), jnp.int32),
             pltpu.SemaphoreType.DMA((12,)),
-            pltpu.SemaphoreType.DMA((9, n)),
-            pltpu.SemaphoreType.DMA((9, n)),
-            pltpu.SemaphoreType.DMA((2, everyone)),
-            pltpu.SemaphoreType.DMA((2, everyone)),
-            pltpu.SemaphoreType.DMA((n // inner,)),
-            pltpu.SemaphoreType.DMA((n // inner,)),
-            pltpu.SemaphoreType.DMA((reps,)),
-            pltpu.SemaphoreType.DMA((reps,)),
+            pltpu.SemaphoreType.DMA((10,)),
+            pltpu.SemaphoreType.DMA((10,)),
+            pltpu.SemaphoreType.DMA((2,)),
+            pltpu.SemaphoreType.DMA((2,)),
+            pltpu.SemaphoreType.DMA,
+            pltpu.SemaphoreType.DMA,
+            pltpu.SemaphoreType.DMA,
+            pltpu.SemaphoreType.DMA,
         ],
         compiler_params=pltpu.CompilerParams(
             collective_id=0, has_side_effects=True, vmem_limit_bytes=40 * 1024 * 1024

time: 82.4 us -> 80.8 us (0.981)
  Pallas kernels: 81 us -> 79.4 us
    pallas_call x1, Pallas kernels: 80 us -> 78.4 us  [fused(): pl.pallas_call(functools.partial(step_kernel, n, reps, inner), out_shape=...]
where the time goes in v4:
time: 80.8 us; the launch traced here: 80.6 us
  Pallas kernels  79.4 us (98%)
  between operations  0.94 us (1%)
    pallas_call x1, Pallas kernels, fused(): pl.pallas_call(functools.partial(step_kernel, n, reps, inner), out_shape=...  78.4 us

profile of v4, /device:TPU:0, one launch (start us, length us, event | category | flops | bytes accessed | tf_op | source)
XLA Modules:
  0.0 80.6 jit_solution(11750255063877372031)
XLA Ops:
  0.6 0.0 copy-start.3
  0.6 0.0 copy-start.4
  0.7 0.0 copy-start.5
  0.7 0.0 copy-start.6
  0.7 0.0 copy-start.7
  0.7 0.0 copy-start.8
  0.7 0.0 copy-start.9
  0.7 78.4 %shard_map.136 = (bf16[1024,256]{1,0:T(8,128)(2,1)S(1)}, bf16[1024,256]{1,0:T(8,128)(2,1)S(1)}, f32[256,256]{1,0:T(8,128)S(1)}, s32[1]{0:T(128)S(4)}) custom-call(bf16[1024,256]{1,0:T(8,128)(2,1)} %features_hbm.1, bf16[1024,256]{1,0:T(8,128)(2,1)} %history_hbm.1, s32[1,8]{1,0:T(1,128)} %new_owner_hbm.1, s32[8,1,128]{2,1,0:T(1,128)} %bitcast.21.pulls_hbm, ...), custom_call_target="tpu_custom_call" | custom-call | tf_op jit(solution)/shard_map/pallas_call | solution.py:704
  79.1 0.0 copy-done.3
  79.1 0.0 copy-done.4
  79.1 0.0 copy-done.5
  79.1 0.0 copy-done.6
  79.1 0.0 copy-done.7
  79.1 0.0 copy-done.8
  79.1 0.0 copy-done.9
  79.1 1.3 %conditional.1 = ((bf16[1024,256]{1,0:T(8,128)(2,1)}, bf16[1024,256]{1,0:T(8,128)(2,1)}, f32[256,256]{1,0:T(8,128)})) conditional(s32[]{:T(128)} %bitcast.24, (bf16[1024,256]{1,0:T(8,128)(2,1)S(1)}, bf16[1024,256]{1,0:T(8,128)(2,1)S(1)}, f32[256,256]{1,0:T(8,128)S(1)}) %tuple.13, (s32[8,16]{1,0:T(8,128)S(1)}, bf16[1024,1024]{1,0:T(8,128)(2,1)}, ...), branch_computations={%region_0.0_spmd, %region_1.0_spmd} | conditional | flops 4706077696 | bytes 95291976 | solution.py:852
  79.2 1.1 %branch_0_fun.1 = (bf16[1024,256]{1,0:T(8,128)(2,1)}, bf16[1024,256]{1,0:T(8,128)(2,1)}, f32[256,256]{1,0:T(8,128)}) custom-call(bf16[1024,256]{1,0:T(8,128)(2,1)S(1)} %get-tuple-element.28.refs_0_, bf16[1024,256]{1,0:T(8,128)(2,1)S(1)} %get-tuple-element.29.refs_1_, f32[256,256]{1,0:T(8,128)S(1)} %get-tuple-element.30.refs_2_), custom_call_target="tpu_custom_call" | custom-call | tf_op jit(solution)/shard_map/cond/branch_0_fun/pallas_call | solution.py:659
Async XLA Ops:
  0.6 78.4 %copy-start.3 = (bf16[1024,256]{1,0:T(8,128)(2,1)S(1)}, bf16[1024,256]{1,0:T(8,128)(2,1)}, u32[]{:S(2)}) copy-start(bf16[1024,256]{1,0:T(8,128)(2,1)} %features_hbm.1) | copy-start | bytes 1572868
  0.6 78.4 %copy-start.4 = (bf16[1024,256]{1,0:T(8,128)(2,1)S(1)}, bf16[1024,256]{1,0:T(8,128)(2,1)}, u32[]{:S(2)}) copy-start(bf16[1024,256]{1,0:T(8,128)(2,1)} %history_hbm.1) | copy-start | bytes 1572868
  0.7 78.4 %copy-start.5 = (bf16[256,256]{1,0:T(8,128)(2,1)S(1)}, bf16[256,256]{1,0:T(8,128)(2,1)}, u32[]{:S(2)}) copy-start(bf16[256,256]{1,0:T(8,128)(2,1)} %w_second_hbm.1) | copy-start | bytes 393220
  0.7 78.4 %copy-start.6 = (bf16[256,256]{1,0:T(8,128)(2,1)S(1)}, bf16[256,256]{1,0:T(8,128)(2,1)}, u32[]{:S(2)}) copy-start(bf16[256,256]{1,0:T(8,128)(2,1)} %w_first_hbm.1) | copy-start | bytes 393220
  0.7 78.4 %copy-start.7 = (s32[8,16]{1,0:T(8,128)S(1)}, s32[8,16]{1,0:T(8,128)}, u32[]{:S(2)}) copy-start(s32[8,16]{1,0:T(8,128)} %occupancy_hbm.1) | copy-start | bytes 1540
  0.7 78.4 %copy-start.8 = (f32[256]{0:T(256)S(1)}, f32[256]{0:T(256)}, u32[]{:S(2)}) copy-start(f32[256]{0:T(256)} %param.21) | copy-start | bytes 3076
  0.7 78.4 %copy-start.9 = (s32[1,8]{1,0:T(1,128)S(1)}, s32[1,8]{1,0:T(1,128)}, u32[]{:S(2)}) copy-start(s32[1,8]{1,0:T(1,128)} %new_owner_hbm.1) | copy-start | bytes 100
